TPU v7x, 64 devices: a 2x2x8 block of a 4x4x8 slice. The times are simulated.
64 devices in a mesh: rep: 4 (over x, y), dp: 16 (over z, core).
Axes of the slice: x: 2, y: 2, z: 8, core: 2. Of those that a mesh axis runs over, the one named last changes fastest.
The devices are a block of a 4x4x8 slice.
Arguments:
- x: bfloat16 [64, 1024, 640], P(('rep', 'dp')), parts along dimension 0
- dy: bfloat16 [64, 1024, 640], P(('rep', 'dp')), parts along dimension 0
- w_gate: bfloat16 [2, 640, 3456], P(None, 'dp')
- w_up: bfloat16 [2, 640, 3456], P(None, 'dp')
- w_down: bfloat16 [2, 3456, 640], P(None, 'dp')
- m_w_gate: float32 [2, 640, 3456], P(None, 'dp')
- m_w_up: float32 [2, 640, 3456], P(None, 'dp')
- m_w_down: float32 [2, 3456, 640], P(None, 'dp')
- v_w_gate: float32 [2, 640, 3456], P(None, 'dp')
- v_w_up: float32 [2, 640, 3456], P(None, 'dp')
- v_w_down: float32 [2, 3456, 640], P(None, 'dp')
Outputs:
- output 1: bfloat16 [8, 640, 3456], P('rep', 'dp'), parts along dimension 0
- output 2: bfloat16 [8, 640, 3456], P('rep', 'dp'), parts along dimension 0
- output 3: bfloat16 [8, 3456, 640], P('rep', 'dp'), parts along dimension 0
- output 4: float32 [8, 640, 3456], P('rep', 'dp'), parts along dimension 0
- output 5: float32 [8, 640, 3456], P('rep', 'dp'), parts along dimension 0
- output 6: float32 [8, 3456, 640], P('rep', 'dp'), parts along dimension 0
- output 7: float32 [8, 640, 3456], P('rep', 'dp'), parts along dimension 0
- output 8: float32 [8, 640, 3456], P('rep', 'dp'), parts along dimension 0
- output 9: float32 [8, 3456, 640], P('rep', 'dp'), parts along dimension 0
There are 4 independent parts. A program takes and returns all parts, laid end to end along the dimension named above; an argument that names none is the same for every part.
All inputs are finite; a program needn't handle non-finite values.
Results may differ from a plain program's by a relative error of at most 0.0224.
Values are sent between devices in bfloat16 or wider.
A program may use at most 768 MiB of HBM per device.

v0:
```python
import jax
import jax.numpy as jnp
from jax import lax
from jax.sharding import PartitionSpec as P

NAMES = ("w_gate", "w_up", "w_down")


def matmul(a, w):
    return jnp.dot(a, w, preferred_element_type=jnp.float32).astype(jnp.bfloat16)


def normed(h):
    wide = h.astype(jnp.float32)
    scale = lax.rsqrt(jnp.mean(wide**2, -1, keepdims=True) + 1e-6)
    return (wide * scale).astype(jnp.bfloat16)


def layer(h, w):
    a = normed(h)
    gate = jnp.dot(a, w["w_gate"], preferred_element_type=jnp.float32)
    up = jnp.dot(a, w["w_up"], preferred_element_type=jnp.float32)
    return h + matmul((jax.nn.silu(gate) * up).astype(jnp.bfloat16), w["w_down"])


def adamw(w, m, v, g):
    m = 0.9 * m + 0.1 * g
    v = 0.95 * v + 0.05 * g * g
    step = m * lax.rsqrt(v + 1e-8) + 0.1 * w
    return (w - 0.02 * step).astype(jnp.bfloat16), m, v


def clipped(gradients, sum_of_squares, count):
    factor = jnp.minimum(1.0, 0.5 * lax.rsqrt(sum_of_squares / count + 1e-30))
    return [g * factor for g in gradients]


def solution(mesh):
    def fetched(weights, number):
        return {name: lax.all_gather(w[number], "dp", axis=0, tiled=True) for name, w in zip(NAMES, weights, strict=True)}

    def step(x, dy, *arrays):
        weights, m, v = (arrays[i : i + 3] for i in (0, 3, 6))
        layers = weights[0].shape[0]
        h, kept = x[0], []
        for number in range(layers):
            kept.append(h)
            h = layer(h, fetched(weights, number))
        by_h, mine = dy[0], [None] * layers
        for number in reversed(range(layers)):
            _, back = jax.vjp(lambda w, h: layer(h, w), fetched(weights, number), kept[number])
            by_w, by_h = back(by_h)
            mine[number] = [lax.psum_scatter(by_w[name], "dp", scatter_dimension=0, tiled=True) for name in NAMES]
        gradients = [jnp.stack([mine[number][i] for number in range(layers)]).astype(jnp.float32) for i in range(3)]
        squares = lax.psum(sum(jnp.sum(g * g) for g in gradients), "dp")
        gradients = clipped(gradients, squares, lax.psum(1, "dp") * sum(g.size for g in gradients))
        new = [adamw(w.astype(jnp.float32), m, v, g) for w, m, v, g in zip(weights, m, v, gradients, strict=True)]
        return tuple(one[which] for which in range(3) for one in new)

    states, cut = P(("rep", "dp"), None, None), P(None, "dp", None)
    return jax.shard_map(
        step,
        mesh=mesh,
        in_specs=(states, states) + (cut,) * 9,
        out_specs=(P("rep", "dp", None),) * 9,
        check_vma=False,
    )
```

profile of v0, /device:TPU:21, one launch (start us, length us, event | category | flops | bytes accessed | tf_op | source)
XLA Modules:
  0.0 724.8 jit_solution(16034325949101259140)
XLA Ops:
  17.8 36.6 %all-gather.13.cloned.1.call-done = bf16[1,640,3456]{2,1,0:T(8,128)(2,1)} async-done(((bf16[1,40,3456]{2,1,0:T(8,128)(2,1)}), bf16[1,640,3456]{2,1,0:T(8,128)(2,1)}) %all-gather.13.cloned.1.call-update) | async-done | bytes 4423696 | tf_op jit(solution)/shard_map/all_gather | solution.py:40
  54.3 11.3 %fusion.34 = f32[1024,3456]{1,0:T(8,128)} fusion(bf16[1,640,3456]{2,1,0:T(8,128)(2,1)} %all-gather.13.cloned.1.call-done, bf16[1,1024,640]{1,2,0:T(8,128)(2,1)S(1)} %copy.22, f32[1024]{0:T(1024)S(1)} %add_rsqrt_fusion), kind=kOutput, calls=%fused_computation.49 | convolution fusion | flops 4531814400 | bytes 19894272 | tf_op jit(solution)/shard_map/dot_general | solution.py:21
  65.7 28.5 %all-gather.15.cloned.1.call-done = bf16[1,640,3456]{2,1,0:T(8,128)(2,1)} async-done(((bf16[1,40,3456]{2,1,0:T(8,128)(2,1)}), bf16[1,640,3456]{2,1,0:T(8,128)(2,1)}) %all-gather.15.cloned.1.call-update) | async-done | bytes 4423696 | tf_op jit(solution)/shard_map/all_gather | solution.py:40
  94.1 16.3 %multiply_convert_fusion.1 = (bf16[1024,3456]{1,0:T(8,128)(2,1)}, f32[1024,3456]{1,0:T(8,128)}) fusion(f32[1024,3456]{1,0:T(8,128)} %fusion.34, bf16[1,640,3456]{2,1,0:T(8,128)(2,1)} %all-gather.15.cloned.1.call-done, bf16[1,1024,640]{1,2,0:T(8,128)(2,1)S(1)} %copy.22, f32[1024]{0:T(1024)S(1)} %add_rsqrt_fusion), kind=kOutput, calls=%fused_computation.17 | convolution fusion | flops 4553048064 | bytes 41127936 | tf_op jit(solution)/shard_map/dot_general | solution.py:22
  110.4 23.5 %all-gather.17.cloned.1.call-done = bf16[1,3456,640]{2,1,0:T(8,128)(2,1)} async-done(((bf16[1,216,640]{2,1,0:T(8,128)(2,1)}), bf16[1,3456,640]{2,1,0:T(8,128)(2,1)}) %all-gather.17.cloned.1.call-update) | async-done | bytes 4423696 | tf_op jit(solution)/shard_map/all_gather | solution.py:40
  143.3 30.3 %all-gather.21.cloned.1.call-done = bf16[1,3456,640]{2,1,0:T(8,128)(2,1)} async-done(((bf16[1,216,640]{2,1,0:T(8,128)(2,1)}), bf16[1,3456,640]{2,1,0:T(8,128)(2,1)}) %all-gather.21.cloned.1.call-update) | async-done | bytes 4423696 | tf_op jit(solution)/shard_map/all_gather | solution.py:40
  173.6 10.3 %convolution_convert_fusion.1 = bf16[1024,3456]{1,0:T(8,128)(2,1)} fusion(bf16[1,3456,640]{2,1,0:T(8,128)(2,1)} %all-gather.21.cloned.1.call-done, bf16[1,1024,640]{2,1,0:T(8,128)(2,1)} %param.12), kind=kOutput, calls=%fused_computation.23 | convolution fusion | flops 4533387264 | bytes 12812288 | tf_op jit(solution)/shard_map/transpose(jvp())/dot_general | solution.py:10
  183.9 29.4 %all-gather.23.cloned.1.call-done = bf16[1,640,3456]{2,1,0:T(8,128)(2,1)} async-done(((bf16[1,40,3456]{2,1,0:T(8,128)(2,1)}), bf16[1,640,3456]{2,1,0:T(8,128)(2,1)}) %all-gather.23.cloned.1.call-update) | async-done | bytes 4423696 | tf_op jit(solution)/shard_map/all_gather | solution.py:40
  213.3 11.2 %fusion.21 = f32[1024,3456]{1,0:T(8,128)} fusion(bf16[1,640,3456]{2,1,0:T(8,128)(2,1)} %all-gather.23.cloned.1.call-done, bf16[1024,640]{0,1:T(8,128)(2,1)S(1)} %get-tuple-element.27, f32[1024]{0:T(1024)S(1)} %fusion.90), kind=kOutput, calls=%fused_computation.36 | convolution fusion | flops 4531814400 | bytes 19894272 | tf_op jit(solution)/shard_map/jvp()/dot_general | solution.py:22
  224.5 28.5 %all-gather.19.cloned.1.call-done = bf16[1,640,3456]{2,1,0:T(8,128)(2,1)} async-done(((bf16[1,40,3456]{2,1,0:T(8,128)(2,1)}), bf16[1,640,3456]{2,1,0:T(8,128)(2,1)}) %all-gather.19.cloned.1.call-update) | async-done | bytes 4423696 | tf_op jit(solution)/shard_map/all_gather | solution.py:40
  253.0 20.0 %fusion.2 = (bf16[1024,3456]{1,0:T(8,128)(2,1)}, f32[1024,3456]{1,0:T(8,128)}) fusion(f32[1024,3456]{1,0:T(8,128)} %fusion.21, bf16[1024,3456]{1,0:T(8,128)(2,1)} %convolution_convert_fusion.1, bf16[1,640,3456]{2,1,0:T(8,128)(2,1)} %all-gather.19.cloned.1.call-done, bf16[1024,640]{0,1:T(8,128)(2,1)S(1)} %get-tuple-element.27, f32[1024]{0:T(1024)S(1)} %fusion.90), kind=kOutput, calls=%fused_computation.8 | convolution fusion | flops 4574281728 | bytes 48205824 | tf_op jit(solution)/shard_map/jvp()/dot_general | solution.py:21
  273.0 11.2 %fusion.50 = bf16[1024,640]{0,1:T(8,128)(2,1)S(1)} fusion(bf16[1,640,3456]{2,1,0:T(8,128)(2,1)} %all-gather.23.cloned.1.call-done, bf16[1024,3456]{1,0:T(8,128)(2,1)} %convolution_convert_fusion.1, f32[1024,3456]{1,0:T(8,128)} %get-tuple-element.29), kind=kOutput, calls=%fused_computation.66 | convolution fusion | flops 4551737344 | bytes 26968064 | tf_op jit(solution)/shard_map/transpose(jvp())/dot_general | solution.py:22
  291.8 10.4 %convolution_convert_fusion.2 = bf16[3456,640]{1,0:T(8,128)(2,1)} fusion(bf16[1024,3456]{1,0:T(8,128)(2,1)} %get-tuple-element.24, bf16[1024,640]{0,1:T(8,128)(2,1)S(1)} %fusion.56), kind=kOutput, calls=%fused_computation.30 | convolution fusion | flops 4532060160 | bytes 12812288 | tf_op jit(solution)/shard_map/transpose(jvp())/dot_general | solution.py:10
  303.6 18.0 %fusion.15 = bf16[3456,640]{1,0:T(8,128)(2,1)} fusion(f32[1024,3456]{1,0:T(8,128)} %fusion.21, bf16[1,1024,640]{2,1,0:T(8,128)(2,1)S(1)} %copy-done.9, f32[1024,3456]{1,0:T(8,128)} %get-tuple-element.29), kind=kOutput, calls=%fused_computation.26 | convolution fusion | flops 4553293824 | bytes 34045952 | tf_op jit(solution)/shard_map/transpose(jvp())/dot_general | solution.py:10
  333.4 10.4 %fusion.20 = bf16[640,3456]{1,0:T(8,128)(2,1)} fusion(bf16[1024,3456]{1,0:T(8,128)(2,1)S(1)} %convolution_convert_fusion, f32[1024,3456]{1,0:T(8,128)} %fusion.34, bf16[1,1024,640]{1,2,0:T(8,128)(2,1)S(1)} %copy-done.1, f32[1024]{0:T(1024)S(1)} %copy-done.20), kind=kOutput, calls=%fused_computation.29 | convolution fusion | flops 4555259904 | bytes 26972160 | tf_op jit(solution)/shard_map/transpose(jvp())/dot_general | solution.py:22
  344.0 11.4 %fusion.16 = bf16[640,3456]{1,0:T(8,128)(2,1)} fusion(bf16[1024,3456]{1,0:T(8,128)(2,1)} %convolution_convert_fusion.1, bf16[1024,640]{0,1:T(8,128)(2,1)S(1)} %get-tuple-element.27, f32[1024]{0:T(1024)S(1)} %fusion.90, f32[1024,3456]{1,0:T(8,128)} %get-tuple-element.29), kind=kOutput, calls=%fused_computation.27 | convolution fusion | flops 4555259904 | bytes 26972160 | tf_op jit(solution)/shard_map/transpose(jvp())/dot_general | solution.py:22
  355.5 16.7 %fusion.17 = bf16[640,3456]{1,0:T(8,128)(2,1)} fusion(f32[1024,3456]{1,0:T(8,128)} %fusion.34, f32[1024,3456]{1,0:T(8,128)} %get-tuple-element.25, bf16[1024,3456]{1,0:T(8,128)(2,1)} %copy-done.23, bf16[1,1024,640]{1,2,0:T(8,128)(2,1)S(1)} %copy-done.1, f32[1024]{0:T(1024)S(1)} %copy-done.20), kind=kOutput, calls=%fused_computation.28 | convolution fusion | flops 4572954624 | bytes 41127936 | tf_op jit(solution)/shard_map/transpose(jvp())/dot_general | solution.py:21
  372.3 9.5 %convolution_convert_fusion.3 = bf16[640,3456]{1,0:T(8,128)(2,1)} fusion(bf16[1024,3456]{1,0:T(8,128)(2,1)} %get-tuple-element.28, bf16[1024,640]{0,1:T(8,128)(2,1)S(1)} %get-tuple-element.27, f32[1024]{0:T(1024)S(1)} %fusion.90), kind=kOutput, calls=%fused_computation.31 | convolution fusion | flops 4531814400 | bytes 12816384 | tf_op jit(solution)/shard_map/transpose(jvp())/dot_general | solution.py:21
  381.9 41.7 %reduce-scatter.29.cloned.1.call-done = bf16[216,640]{1,0:T(8,128)(2,1)} async-done(((bf16[3456,640]{1,0:T(8,128)(2,1)}), bf16[216,640]{1,0:T(8,128)(2,1)}) %reduce-scatter.29.cloned.1.call-update) | async-done | bytes 276496
  425.6 61.7 %reduce-scatter.23.cloned.1.call-done = bf16[40,3456]{1,0:T(8,128)(2,1)} async-done(((bf16[640,3456]{1,0:T(8,128)(2,1)}), bf16[40,3456]{1,0:T(8,128)(2,1)}) %reduce-scatter.23.cloned.1.call-update) | async-done | bytes 276496
  487.2 63.5 %reduce-scatter.25.cloned.1.call-done = bf16[40,3456]{1,0:T(8,128)(2,1)} async-done(((bf16[640,3456]{1,0:T(8,128)(2,1)}), bf16[40,3456]{1,0:T(8,128)(2,1)}) %reduce-scatter.25.cloned.1.call-update) | async-done | bytes 276496
  552.6 61.7 %reduce-scatter.19.cloned.1.call-done = bf16[40,3456]{1,0:T(8,128)(2,1)} async-done(((bf16[640,3456]{1,0:T(8,128)(2,1)}), bf16[40,3456]{1,0:T(8,128)(2,1)}) %reduce-scatter.19.cloned.1.call-update) | async-done | bytes 276496
  614.3 63.5 %reduce-scatter.21.cloned.1.call-done = bf16[40,3456]{1,0:T(8,128)(2,1)} async-done(((bf16[640,3456]{1,0:T(8,128)(2,1)}), bf16[40,3456]{1,0:T(8,128)(2,1)}) %reduce-scatter.21.cloned.1.call-update) | async-done | bytes 276496
  681.7 27.4 %psum.7 = f32[]{:T(128)} all-reduce(f32[]{:T(128)S(6)} %add.99), channel_id=1, replica_groups=mesh['rep'=4,'dp'=16] {'dp'}, use_global_device_ids=true, to_apply=%region_12.13 | all-reduce | flops 1 | bytes 8 | tf_op jit(solution)/shard_map/psum | solution.py:55
  (91 shorter events, 54.3 us)
Async XLA Ops:
  7.2 4.2 copy-start.3
  7.2 47.1 %all-gather.13.cloned.1.call-start = ((), (), s32[]{:S(2)}) async-start(), calls=%async_computation.6 | async-start | bytes 4700160 | tf_op jit(solution)/shard_map/all_gather | solution.py:40
  9.3 84.9 %all-gather.15.cloned.1.call-start = ((), (), s32[]{:S(2)}) async-start(), calls=%async_computation.7 | async-start | bytes 4700160 | tf_op jit(solution)/shard_map/all_gather | solution.py:40
  11.3 122.7 %all-gather.17.cloned.1.call-start = ((), (), s32[]{:S(2)}) async-start(), calls=%async_computation.8 | async-start | bytes 4700160 | tf_op jit(solution)/shard_map/all_gather | solution.py:40
  12.2 4.0 copy-start.8
  12.3 161.4 %all-gather.21.cloned.1.call-start = ((), (), s32[]{:S(2)}) async-start(), calls=%async_computation.10 | async-start | bytes 4700160 | tf_op jit(solution)/shard_map/all_gather | solution.py:40
  12.9 200.4 %all-gather.23.cloned.1.call-start = ((), (), s32[]{:S(2)}) async-start(), calls=%async_computation.11 | async-start | bytes 4700160 | tf_op jit(solution)/shard_map/all_gather | solution.py:40
  13.5 239.4 %all-gather.19.cloned.1.call-start = ((), (), s32[]{:S(2)}) async-start(), calls=%async_computation.9 | async-start | bytes 4700160 | tf_op jit(solution)/shard_map/all_gather | solution.py:40
  14.2 367.7 %reduce-scatter.27.cloned.1.call-start = ((), (), s32[]{:S(2)}) async-start(), calls=%async_computation.16 | async-start | bytes 4700160
  15.9 118.1 %copy-start = (bf16[1,1024,640]{1,2,0:T(8,128)(2,1)}, bf16[1,1024,640]{1,2,0:T(8,128)(2,1)S(1)}, u32[]{:S(2)}) copy-start(bf16[1,1024,640]{1,2,0:T(8,128)(2,1)S(1)} %copy.22) | copy-start | bytes 3932164
  16.2 77.9 %copy-start.19 = (f32[1024]{0:T(1024)}, f32[1024]{0:T(1024)S(1)}, u32[]{:S(2)}) copy-start(f32[1024]{0:T(1024)S(1)} %add_rsqrt_fusion) | copy-start | bytes 12292
  273.0 11.2 %copy-start.21 = (bf16[1,640,3456]{2,1,0:T(8,128)(2,1)S(1)}, bf16[1,640,3456]{2,1,0:T(8,128)(2,1)}, u32[]{:S(2)}) copy-start(bf16[1,640,3456]{2,1,0:T(8,128)(2,1)} %all-gather.19.cloned.1.call-done) | copy-start | bytes 13271044
  273.0 11.7 %copy-start.22 = (bf16[1024,3456]{1,0:T(8,128)(2,1)S(1)}, bf16[1024,3456]{1,0:T(8,128)(2,1)}, u32[]{:S(2)}) copy-start(bf16[1024,3456]{1,0:T(8,128)(2,1)} %get-tuple-element.28) | copy-start | bytes 21233668
  284.7 5.1 copy-start.2
  302.3 121.3 %reduce-scatter.29.cloned.1.call-start = ((), (), s32[]{:S(2)}) async-start(), calls=%async_computation.17 | async-start | bytes 4700160
  321.6 11.8 %copy-start.1 = (bf16[1,1024,640]{1,2,0:T(8,128)(2,1)S(1)}, bf16[1,1024,640]{1,2,0:T(8,128)(2,1)}, u32[]{:S(2)}) copy-start(bf16[1,1024,640]{1,2,0:T(8,128)(2,1)} %copy-done) | copy-start | bytes 3932164
  321.6 11.8 %copy-start.20 = (f32[1024]{0:T(1024)S(1)}, f32[1024]{0:T(1024)}, u32[]{:S(2)}) copy-start(f32[1024]{0:T(1024)} %copy-done.19) | copy-start | bytes 12292
  321.6 165.6 %reduce-scatter.23.cloned.1.call-start = ((), (), s32[]{:S(2)}) async-start(), calls=%async_computation.14 | async-start | bytes 4700160
  343.9 206.8 %reduce-scatter.25.cloned.1.call-start = ((), (), s32[]{:S(2)}) async-start(), calls=%async_computation.15 | async-start | bytes 4700160
  355.4 258.9 %reduce-scatter.19.cloned.1.call-start = ((), (), s32[]{:S(2)}) async-start(), calls=%async_computation.12 | async-start | bytes 4700160
  372.3 305.5 %reduce-scatter.21.cloned.1.call-start = ((), (), s32[]{:S(2)}) async-start(), calls=%async_computation.13 | async-start | bytes 4700160
  381.8 327.9 %copy-start.4 = (bf16[2,216,640]{2,1,0:T(8,128)(2,1)S(1)}, bf16[2,216,640]{2,1,0:T(8,128)(2,1)}, u32[]{:S(2)}) copy-start(bf16[2,216,640]{2,1,0:T(8,128)(2,1)} %param.15) | copy-start | bytes 1658884
  381.8 327.9 %copy-start.14 = (f32[2,216,640]{2,1,0:T(8,128)S(1)}, f32[2,216,640]{2,1,0:T(8,128)}, u32[]{:S(2)}) copy-start(f32[2,216,640]{2,1,0:T(8,128)} %param.21) | copy-start | bytes 3317764
  381.8 327.9 %copy-start.15 = (f32[2,216,640]{2,1,0:T(8,128)S(1)}, f32[2,216,640]{2,1,0:T(8,128)}, u32[]{:S(2)}) copy-start(f32[2,216,640]{2,1,0:T(8,128)} %param.18) | copy-start | bytes 3317764
  (12 other events, 33.7 us)
Sparse Core Ops, SparseCore 0:
  10.2 44.0 all-gather.12
  56.5 37.5 all-gather.14
  96.4 37.5 all-gather.16
  136.0 37.5 all-gather.20
  175.7 37.5 all-gather.22
  215.4 37.5 all-gather.18
  302.4 57.5 reduce-scatter.26
  362.4 61.1 reduce-scatter.28
  426.0 61.1 reduce-scatter.22
  489.5 61.1 reduce-scatter.24
  553.1 61.1 reduce-scatter.18
  616.5 61.1 reduce-scatter.20
where the time goes:
time: 732 us; the launch traced here: 725 us
  waiting for transfers between devices  471 us (64%)
  matrix products  180 us (25%)
  blocking collectives  27.4 us (4%)
  between operations  17.6 us (2%)
  other arithmetic  14.4 us (2%)
  local copies, waits for them, and re-layouts  13.7 us (2%)
    unnamed x18, waiting for transfers between devices  294 us
    all_gather x6, waiting for transfers between devices, fetched(): lax.all_gather(w[number], 'dp', axis=0, tiled=True)  177 us
    dot_general x5, matrix products, layer(): gate = jnp.dot(a, w['w_gate'], preferred_element_type=jnp.float32)  62.6 us
    dot_general x5, matrix products, layer(): up = jnp.dot(a, w['w_up'], preferred_element_type=jnp.float32)  60.5 us
    dot_general x5, matrix products, matmul(): jnp.dot(a, w, preferred_element_type=jnp.float32).astype(jnp.bfloat16)  56.9 us
    psum x1, blocking collectives, step(): squares = lax.psum(sum((jnp.sum(g * g) for g in gradients)), 'dp')  27.4 us
  transfers between devices with their start and end apart: 12, of which 11 were waited for; matrix products, arithmetic and copies ran while one was open for 20% of the time, Pallas kernels for 0%

commit v1 on v0

v1 whole, which is shorter than its diff:
```python
import functools

import jax
import jax.numpy as jnp
from jax import lax
from jax.experimental import pallas as pl
from jax.experimental.pallas import tpu as pltpu
from jax.sharding import PartitionSpec as P

MESH = pl.DeviceIdType.MESH
ANY = pl.BlockSpec(memory_space=pltpu.HBM)
F32, BF16 = jnp.float32, jnp.bfloat16
SK = 2
SLOTS = 8
GSLOTS = 16
RSLOTS = 8
DCH = 3
CHUNKS = 9
PIECES = 9


def mm(a, b):
    return jnp.dot(a, b, preferred_element_type=F32)


def mm_nt(a, b):
    return lax.dot_general(a, b, (((1,), (1,)), ((), ())), preferred_element_type=F32)


def mm_tn(a, b):
    return lax.dot_general(a, b, (((0,), (0,)), ((), ())), preferred_element_type=F32)


def train_kernel(nz, x, dy, wg, wu, wd, ggu, gd, sqo, WGU, WD,
                 H, DY, A, AT, DACC, WC, WDC, DGU, ACT, TS, R, TD, RD, BG, BD, FG, FD, SQ, SQALL, sgu, sd,
                 load_sem, w_sem, own_sem, g_recv, g_sib, g_send,
                 r_send, r_recv, ring_send, ring_recv, fin_send, fin_recv, sq_send, sq_recv):
    me = lax.axis_index("dp")
    z, c = me // 2, me % 2
    n = 2 * nz
    half = nz // 2
    tokens, d = H.shape
    rgu = d // n
    cw = TS.shape[-1]
    ff = cw * CHUNKS
    rd = ff // n
    drow = rd // DCH
    crd = 2 * rd
    prow = crd // PIECES
    items = (PIECES + 1) // 2
    per = CHUNKS + items
    total = 2 * per
    gper = DCH + CHUNKS
    gtotal = 2 * gper
    gdone = SK * half + 2
    UF = DCH + gdone + 1
    U1 = gper + DCH + gdone + 1
    U2 = U1 + CHUNKS + 1

    def dev(zz, cc):
        return {"dp": lax.rem(zz + nz, nz) * 2 + cc}

    def remote(src, dst, s, r, to):
        return pltpu.make_async_remote_copy(src, dst, s, r, device_id=to, device_id_type=MESH)

    def wait(ref, sem):
        remote(ref, ref, sem, sem, dev(z, 1 - c)).wait_recv()

    first = [pltpu.make_async_copy(x, H, load_sem.at[0]), pltpu.make_async_copy(dy, DY, load_sem.at[1]), pltpu.make_async_copy(wd, sd, load_sem.at[2])]
    for cp in first:
        cp.start()
    for j in range(CHUNKS):
        for m, w in enumerate((wg, wu)):
            pltpu.make_async_copy(w.at[:, :, j * cw : (j + 1) * cw], sgu.at[:, :, (2 * j + m) * cw : (2 * j + m + 1) * cw], load_sem.at[3]).start()

    barrier = pltpu.get_barrier_semaphore()
    for i in range(1, n):
        pl.semaphore_signal(barrier, inc=1, device_id={"dp": lax.rem(me + i, n)}, device_id_type=MESH)
    pl.semaphore_wait(barrier, n - 1)
    for cp in first:
        cp.wait()
    pltpu.make_async_copy(WGU.at[:, :rgu, :], sgu, load_sem.at[3]).wait()

    SQ[...] = jnp.zeros_like(SQ)

    def normalize(src, transposed):
        def rows(i, _):
            rs = pl.ds(pl.multiple_of(i * 128, 128), 128)
            wide = src[rs, :].astype(F32)
            a = (wide * lax.rsqrt(jnp.mean(wide * wide, -1, keepdims=True) + 1e-6)).astype(BF16)
            A[rs, :] = a
            if transposed:
                AT[:, rs] = a.T
            return 0
        lax.fori_loop(0, tokens // 128, rows, 0)

    def piece(q, src_z, own, fn):
        layer, r = q // gper, q % gper
        blk = lax.rem(src_z + nz, nz) * 2 + c
        @pl.when(r < DCH)
        def _():
            dst = WD.at[layer, pl.ds(pl.multiple_of(blk * rd + r * drow, 8), drow), :]
            fn(sd.at[layer, pl.ds(pl.multiple_of(r * drow, 8), drow), :] if own else dst, dst)
        @pl.when(r >= DCH)
        def _():
            cs = pl.ds(pl.multiple_of((r - DCH) * 2 * cw, 128), 2 * cw)
            dst = WGU.at[layer, pl.ds(pl.multiple_of(blk * rgu, 8), rgu), cs]
            fn(sgu.at[layer, :, cs] if own else dst, dst)

    def to_sibling(q, src, dst):
        remote(src, dst, g_send.at[q % GSLOTS], g_sib.at[q % GSLOTS], dev(z, 1 - c)).start()

    def to_next(q, way, hop, src, dst):
        to = z + 1 if way == 0 else z - 1
        remote(src, dst, g_send.at[q % GSLOTS], g_recv.at[way, hop - 1, q % RSLOTS], dev(to, c)).start()

    def gather_step(t):
        @pl.when(t < gtotal)
        def _():
            def own(src, dst):
                to_next(t, 0, 1, src, dst)
                to_next(t, 1, 1, src, dst)
                to_sibling(t, src, dst)
                pltpu.make_async_copy(src, dst, own_sem.at[t % GSLOTS]).start()
            piece(t, z, True, own)
        for h in range(1, half + 1):
            q = t - SK * h
            for way in (0, 1):
                longer = q % 2 == way
                ok = (q >= 0) & (q < gtotal)
                if h == half:
                    ok = ok & longer
                @pl.when(ok)
                def _():
                    def go(src, dst):
                        remote(src, dst, g_send.at[0], g_recv.at[way, h - 1, q % RSLOTS], dev(z, 1 - c)).wait_recv()
                        if h < half - 1:
                            to_next(q, way, h + 1, src, dst)
                        elif h == half - 1:
                            @pl.when(longer)
                            def _():
                                to_next(q, way, h + 1, src, dst)
                        to_sibling(q, src, dst)
                    piece(q, z - h if way == 0 else z + h, False, go)
        q = t - gdone
        @pl.when((q >= 0) & (q < gtotal))
        def _():
            layer, r, slot = q // gper, q % gper, q % GSLOTS
            def both(ref):
                for rows, sem in ((1, own_sem), (nz, g_sib), (2 * nz - 1, g_send)):
                    a = ref(rows)
                    pltpu.make_async_copy(a, a, sem.at[slot]).wait()
            @pl.when(r < DCH)
            def _():
                both(lambda k: WD.at[layer, pl.ds(0, k * drow), :])
            @pl.when(r >= DCH)
            def _():
                cs = pl.ds(pl.multiple_of((r - DCH) * 2 * cw, 128), 2 * cw)
                both(lambda k: WGU.at[layer, pl.ds(0, k * rgu), cs])

    def work(u):
        k0, k1, k2 = u - UF, u - U1, u - U2
        on = lambda k: (k >= 0) & (k < CHUNKS)
        kind = jnp.where(u < U1, 0, jnp.where(u < U2, 1, 2))
        return on(k0) | on(k1) | on(k2), kind, jnp.where(u < U1, k0, jnp.where(u < U2, k1, k2))

    def weights(u):
        on, kind, j = work(u)
        layer = jnp.where(kind == 1, 1, 0)
        slot = u % 2
        return on, (pltpu.make_async_copy(WGU.at[layer, :, pl.ds(pl.multiple_of(j * 2 * cw, 128), 2 * cw)], WC.at[slot], w_sem.at[slot, 0]),
                    pltpu.make_async_copy(WD.at[layer, pl.ds(pl.multiple_of(j * cw, 128), cw), :], WDC.at[slot], w_sem.at[slot, 1]))

    def forward(j, slot):
        gu = mm(A[...], WC[slot])
        g, up = gu[:, :cw], gu[:, cw:]
        ACT[...] = (g * jax.nn.sigmoid(g) * up).astype(BF16)
        @pl.when(j == 0)
        def _():
            DACC[...] = jnp.zeros_like(DACC)
        DACC[...] += mm(ACT[...], WDC[slot])

    def compute(j, slot):
        gu = mm(A[...], WC[slot])
        g, up = gu[:, :cw], gu[:, cw:]
        back = mm_nt(DY[...], WDC[slot]).astype(BF16).astype(F32)
        sg = jax.nn.sigmoid(g)
        s = g * sg
        ACT[...] = (s * up).astype(BF16)
        DGU[:, :cw] = (back * up * (sg + s * (1.0 - sg))).astype(BF16)
        DGU[:, cw:] = (back * s).astype(BF16)
        t = mm(AT[...], DGU[...]).astype(BF16)
        TS[0, j] = t[:, :cw]
        TS[1, j] = t[:, cw:]

    def compute_rest(kind, j, slot):
        @pl.when(kind == 1)
        def _():
            @pl.when(j == 0)
            def _():
                DACC[...] = jnp.zeros_like(DACC)
            DACC[...] += mm_nt(DGU[...], WC[slot])
        TD[jnp.where(kind == 1, 1, 0), pl.ds(pl.multiple_of(j * cw, 128), cw), :] = mm_tn(ACT[...], DY[...]).astype(BF16)

    def after_forward():
        def rows(i, _):
            rs = pl.ds(pl.multiple_of(i * 128, 128), 128)
            H[rs, :] = (H[rs, :].astype(F32) + DACC[rs, :].astype(BF16).astype(F32)).astype(BF16)
            return 0
        lax.fori_loop(0, tokens // 128, rows, 0)
        normalize(H, True)

    def between():
        xin = pltpu.make_async_copy(x, A, load_sem.at[0])
        xin.start()
        def rows(i, _):
            rs = pl.ds(pl.multiple_of(i * 128, 128), 128)
            wide = H[rs, :].astype(F32)
            scale = lax.rsqrt(jnp.mean(wide * wide, -1, keepdims=True) + 1e-6)
            da = DACC[rs, :].astype(BF16).astype(F32)
            dh = scale * da - wide * (scale * scale * scale * jnp.mean(wide * da, -1, keepdims=True))
            DY[rs, :] = (DY[rs, :].astype(F32) + dh.astype(BF16).astype(F32)).astype(BF16)
            return 0
        lax.fori_loop(0, tokens // 128, rows, 0)
        xin.wait()
        normalize(A, True)

    def item(i):
        return 1 - i // per, i % per

    def piece_of(layer, k, cc):
        return 2 * k + lax.rem(cc + layer, 2)

    def send_terms(i, start):
        layer, r = item(i)
        @pl.when(r < CHUNKS)
        def _():
            cp = remote(TS.at[1 - c, r], R.at[r], r_send, r_recv.at[i], dev(z, 1 - c))
            cp.start() if start else cp.wait_send()
        @pl.when(r >= CHUNKS)
        def _():
            k = r - CHUNKS
            p = piece_of(layer, k, 1 - c)
            @pl.when(p < PIECES)
            def _():
                if start:
                    for zz in range(nz):
                        rs = pl.ds(pl.multiple_of(zz * crd + p * prow, 16), prow)
                        remote(TD.at[layer, rs, :], RD.at[k, zz], r_send, r_recv.at[i], dev(z, 1 - c)).start()
                else:
                    wait(RD.at[k], r_send)

    def terms(i, zz, fn):
        layer, r = item(i)
        zz = lax.rem(zz + 2 * nz, nz)
        @pl.when(r < CHUNKS)
        def _():
            rs = pl.ds(pl.multiple_of(zz * 2 * rgu, 16), 2 * rgu)
            fn(TS.at[c, r, rs, :], R.at[r, rs, :], BG, r % 2, True)
        @pl.when(r >= CHUNKS)
        def _():
            k = r - CHUNKS
            p = piece_of(layer, k, c)
            @pl.when(p < PIECES)
            def _():
                fn(TD.at[layer, pl.ds(pl.multiple_of(zz * crd + p * prow, 16), prow), :], RD.at[k, zz], BD, k % 2, False)

    def ring_copy(i, way, s, buf):
        to = z + 1 if way == 0 else z - 1
        slot = i % SLOTS
        return remote(buf.at[way, s, slot], buf.at[way, s + 1, slot], ring_send.at[way, s, slot], ring_recv.at[way, s, slot], dev(to, c))

    def arrived(i, way, s, buf):
        slot = i % SLOTS
        wait(buf.at[way, s, slot], ring_recv.at[way, s - 1, slot])

    def stage(i, way, s):
        def fn_for(hops):
            def fn(own, other, buf, odd, is_gu):
                mine = (odd == way) if hops == half else (odd != way)
                @pl.when(mine)
                def _():
                    slot = i % SLOTS
                    t = own[...].astype(F32) + other[...].astype(F32)
                    if s > 0:
                        arrived(i, way, s, buf)
                        t = t + buf[way, s, slot].astype(F32)
                    buf[way, s, slot] = t.astype(BF16)
                    ring_copy(i, way, s, buf).start()
            return fn
        for hops in (half, half - 1):
            if s < hops:
                terms(i, z + (hops - s) if way == 0 else z - (hops - s), fn_for(hops))

    def stage_sent(i, way, s):
        def fn(own, other, buf, odd, is_gu):
            def go():
                ring_copy(i, way, s, buf).wait_send()
            if s < half - 1:
                go()
            else:
                pl.when(odd == way)(go)
        terms(i, z, fn)

    def last(i):
        layer, r = item(i)
        slot = i % SLOTS
        def fn(own, other, buf, odd, is_gu):
            def add(hops_up):
                t = own[...].astype(F32) + other[...].astype(F32)
                for way, hops in ((0, hops_up), (1, nz - 1 - hops_up)):
                    arrived(i, way, hops, buf)
                    t = t + buf[way, hops, slot].astype(F32)
                w = t.astype(BF16).astype(F32)
                sq = SQ[...]
                for a in range(w.shape[0] // 8):
                    for b in range(w.shape[1] // 128):
                        v = w[8 * a : 8 * a + 8, 128 * b : 128 * b + 128]
                        sq = sq + v * v
                SQ[...] = sq
                out, rows = (FG, rgu) if is_gu else (FD, prow // 2)
                out[slot, 0] = w[:rows].astype(BF16)
                out[slot, 1] = w[rows:].astype(BF16)
            @pl.when(odd == 0)
            def _():
                add(half)
            @pl.when(odd == 1)
            def _():
                add(half - 1)
            if is_gu:
                cs = pl.ds(pl.multiple_of(r * cw, 128), cw)
                pltpu.make_async_copy(FG.at[slot, c], ggu.at[layer, c, :, cs], fin_send.at[0, slot]).start()
                remote(FG.at[slot, 1 - c], ggu.at[layer, c, :, cs], fin_send.at[1, slot], fin_recv.at[layer, 0], dev(z, 1 - c)).start()
            else:
                p = piece_of(layer, r - CHUNKS, c)
                for b in range(2):
                    k = 2 * p + b
                    dst = gd.at[layer, pl.ds(pl.multiple_of(lax.rem(k, PIECES) * (prow // 2), 8), prow // 2), :]
                    @pl.when(k // PIECES == c)
                    def _():
                        pltpu.make_async_copy(FD.at[slot, b], dst, fin_send.at[b, slot]).start()
                    @pl.when(k // PIECES != c)
                    def _():
                        remote(FD.at[slot, b], dst, fin_send.at[b, slot], fin_recv.at[layer, 1], dev(z, 1 - c)).start()
        terms(i, z, fn)

    def last_sent(i):
        slot = i % SLOTS
        def fn(own, other, buf, odd, is_gu):
            for b in range(2):
                wait((FG if is_gu else FD).at[slot, b], fin_send.at[b, slot])
        terms(i, z, fn)

    def valid(i):
        return (i >= 0) & (i < total)

    def reduce_step(t):
        @pl.when(valid(t - 1))
        def _():
            send_terms(t - 1, False)
        for s in range(half):
            i = t - 2 - SK * s
            @pl.when(valid(i))
            def _():
                for way in (0, 1):
                    stage_sent(i, way, s)
        before = t - 2 - SK * half
        @pl.when(valid(before))
        def _():
            last_sent(before)
        final = t - 1 - SK * half
        @pl.when(valid(final))
        def _():
            last(final)
        for s in reversed(range(half)):
            i = t - 1 - SK * s
            @pl.when(valid(i))
            def _():
                if s == 0:
                    layer, r = item(i)
                    @pl.when(r < CHUNKS)
                    def _():
                        wait(R.at[r], r_recv.at[i])
                    @pl.when((r >= CHUNKS) & (piece_of(layer, r - CHUNKS, c) < PIECES))
                    def _():
                        wait(RD.at[r - CHUNKS], r_recv.at[i])
                for way in (0, 1):
                    stage(i, way, s)

    normalize(H, False)

    def step(u, _):
        t = u - U1
        @pl.when(u < gtotal + gdone)
        def _():
            gather_step(u)
        @pl.when(t >= 0)
        def _():
            reduce_step(t)

        on, kind, j = work(u)
        slot = u % 2
        following, loads = weights(u + 1)
        @pl.when(following)
        def _():
            for cp in loads:
                cp.start()
        @pl.when(u == U1 - 1)
        def _():
            after_forward()
        @pl.when(u == U2 - 1)
        def _():
            between()
        @pl.when(on)
        def _():
            for cp in weights(u)[1]:
                cp.wait()
        @pl.when(on & (kind == 0))
        def _():
            forward(j, slot)
        @pl.when(on & (kind > 0))
        def _():
            compute(j, slot)
        @pl.when(valid(t))
        def _():
            send_terms(t, True)
        @pl.when(on & (kind > 0))
        def _():
            compute_rest(kind, j, slot)
        return 0

    lax.fori_loop(0, U1 + total + SK * half + 2, step, 0)

    for i in range(1, n):
        remote(SQ, SQALL.at[me], sq_send, sq_recv, {"dp": lax.rem(me + i, n)}).start()
    for layer in range(2):
        wait(ggu.at[layer, 0], fin_recv.at[layer, 0])
        even = lax.rem(c + layer, 2) == 0
        @pl.when(even)
        def _():
            wait(gd.at[layer, pl.ds(0, PIECES // 2 * (prow // 2)), :], fin_recv.at[layer, 1])
        @pl.when(jnp.logical_not(even))
        def _():
            wait(gd.at[layer, pl.ds(0, (PIECES + 1) // 2 * (prow // 2)), :], fin_recv.at[layer, 1])
    wait(SQALL.at[pl.ds(0, n - 1)], sq_recv)
    acc = SQ[...]
    for i in range(1, n):
        acc = acc + SQALL[lax.rem(me + i, n)]
    sqo[...] = acc
    wait(SQALL.at[pl.ds(0, n - 1)], sq_send)


def train(mesh, x, dy, w_gate, w_up, w_down):
    n = mesh.shape["dp"]
    nz = n // 2
    half = nz // 2
    tokens, d = x.shape
    layers, rgu, ff = w_gate.shape
    rd = ff // n
    cw = ff // CHUNKS
    prow = 2 * rd // PIECES
    items = (PIECES + 1) // 2
    total = 2 * (CHUNKS + items)
    V, S = pltpu.VMEM, pltpu.SemaphoreType.DMA
    shape = jax.ShapeDtypeStruct
    return pl.pallas_call(
        functools.partial(train_kernel, nz),
        out_shape=(
            shape((layers, 2, rgu, ff), BF16), shape((layers, rd, d), BF16), shape((8, 128), F32),
            shape((layers, d, 2 * ff), BF16), shape((layers, ff, d), BF16),
        ),
        in_specs=[ANY] * 5,
        out_specs=(ANY, ANY, pl.BlockSpec(memory_space=pltpu.VMEM), ANY, ANY),
        scratch_shapes=[
            V((tokens, d), BF16), V((tokens, d), BF16), V((tokens, d), BF16), V((d, tokens), BF16), V((tokens, d), F32),
            V((2, d, 2 * cw), BF16), V((2, cw, d), BF16), V((tokens, 2 * cw), BF16), V((tokens, cw), BF16),
            V((2, CHUNKS, d, cw), BF16), V((CHUNKS, d, cw), BF16), V((layers, ff, d), BF16), V((items, nz, prow, d), BF16),
            V((2, half + 1, SLOTS, 2 * rgu, cw), BF16), V((2, half + 1, SLOTS, prow, d), BF16),
            V((SLOTS, 2, rgu, cw), BF16), V((SLOTS, 2, prow // 2, d), BF16),
            V((8, 128), F32), V((n, 8, 128), F32), V((layers, rgu, 2 * ff), BF16), V((layers, rd, d), BF16),
            S((4,)), S((2, 2)), S((GSLOTS,)), S((2, half, RSLOTS)), S((GSLOTS,)), S((GSLOTS,)),
            S, S((total,)), S((2, half, SLOTS)), S((2, half, SLOTS)), S((2, SLOTS)), S((layers, 2)), S, S,
        ],
        compiler_params=pltpu.CompilerParams(collective_id=0, has_side_effects=True, vmem_limit_bytes=63 * 2**20),
        name="train",
    )(x, dy, w_gate, w_up, w_down)


def adamw(w, m, v, g):
    m = 0.9 * m + 0.1 * g
    v = 0.95 * v + 0.05 * g * g
    step = m * lax.rsqrt(v + 1e-8) + 0.1 * w
    return (w - 0.02 * step).astype(BF16), m, v


def solution(mesh):
    n = mesh.shape["dp"]

    def step(x, dy, *arrays):
        weights, m, v = (arrays[i : i + 3] for i in (0, 3, 6))
        ggu, gd, squares = train(mesh, x[0], dy[0], *weights)[:3]
        gradients = [g.astype(F32) for g in (ggu[:, 0], ggu[:, 1], gd)]
        count = n * sum(g.size for g in gradients)
        factor = jnp.minimum(1.0, 0.5 * lax.rsqrt(jnp.sum(squares) / count + 1e-30))
        new = [adamw(w.astype(F32), m, v, g * factor) for w, m, v, g in zip(weights, m, v, gradients, strict=True)]
        return tuple(one[which] for which in range(3) for one in new)

    states, cut = P(("rep", "dp"), None, None), P(None, "dp", None)
    return jax.shard_map(
        step,
        mesh=mesh,
        in_specs=(states, states) + (cut,) * 9,
        out_specs=(P("rep", "dp", None),) * 9,
        check_vma=False,
    )
```

time: 732 us -> 337 us (0.46)
  waiting for transfers between devices: 471 us -> 0 us
  Pallas kernels: 0 us -> 325 us
  matrix products: 180 us -> 0 us
  blocking collectives: 27.4 us -> 0 us
  between operations: 17.6 us -> 1.43 us
  local copies, waits for them, and re-layouts: 13.7 us -> 0.26 us
    pallas_call x0 -> x1, Pallas kernels: none -> 325 us  [train(): pl.pallas_call(functools.partial(train_kernel, nz), out_shape=(shape((lay...]
    unnamed x18 -> x0, waiting for transfers between devices: 294 us -> none
    dot_general x15 -> x0, matrix products: 180 us -> none  [the longest x5 62.6 us: layer(): gate = jnp.dot(a, w['w_gate'], preferred_element_type=jnp.float32)]
    all_gather x6 -> x0, waiting for transfers between devices: 177 us -> none  [fetched(): lax.all_gather(w[number], 'dp', axis=0, tiled=True)]
    psum x1 -> x0, blocking collectives: 27.4 us -> none  [step(): squares = lax.psum(sum((jnp.sum(g * g) for g in gradients)), 'dp')]
    unnamed x50 -> x14, local copies, waits for them, and re-layouts: 9.06 us -> 0.26 us
  transfers between devices with their start and end apart: 12 -> 0, of which waited for: 11 -> 0; matrix products, arithmetic and copies ran while one was open for 20% -> 0% of each run, Pallas kernels for 0% -> 0%
where the time goes in v1:
time: 337 us; the launch traced here: 336 us
  Pallas kernels  325 us (96%)
  other arithmetic  9.37 us (3%)
    pallas_call x1, Pallas kernels, train(): pl.pallas_call(functools.partial(train_kernel, nz), out_shape=(shape((lay...  325 us
    convert_element_type x2, other arithmetic, adamw(): return ((w - 0.02 * step).astype(BF16), m, v)  8.08 us

profile of v1, /device:TPU:21, one launch (start us, length us, event | category | flops | bytes accessed | tf_op | source)
XLA Modules:
  0.0 336.5 jit_solution(9386346509197955357)
XLA Ops:
  0.6 0.0 copy-start
  0.7 325.4 %train.1 = (bf16[2,2,40,3456]{3,2,1,0:T(8,128)(2,1)}, bf16[2,216,640]{2,1,0:T(8,128)(2,1)}, f32[8,128]{1,0:T(8,128)}, bf16[2,640,6912]{2,1,0:T(8,128)(2,1)}, bf16[2,3456,640]{2,1,0:T(8,128)(2,1)}) custom-call(bf16[1024,640]{1,0:T(8,128)(2,1)} %bitcast.24, bf16[1024,640]{1,0:T(8,128)(2,1)} %bitcast.25, bf16[2,40,3456]{2,1,0:T(8,128)(2,1)} %wg.1, ...), custom_call_target="tpu_custom_call" | custom-call | tf_op jit(solution)/shard_map/train/pallas_call | solution.py:466
  326.1 1.3 reduce_sum.9
  328.1 0.0 copy-done
  328.1 0.0 copy-start.1
  328.1 0.0 copy-start.2
  328.1 0.0 copy-start.3
  328.1 0.0 copy-start.4
  328.1 0.0 copy-start.5
  328.1 0.0 copy-start.6
  328.2 3.7 %fusion.8 = (bf16[2,216,640]{2,1,0:T(8,128)(2,1)}, f32[2,216,640]{2,1,0:T(8,128)}, f32[2,216,640]{2,1,0:T(8,128)}) fusion(bf16[2,216,640]{2,1,0:T(8,128)(2,1)S(1)} %copy-done, f32[]{:T(128)S(6)} %min_shard_map.3, bf16[2,216,640]{2,1,0:T(8,128)(2,1)} %get-tuple-element.14, f32[2,216,640]{2,1,0:T(8,128)} %param.21, f32[2,216,640]{2,1,0:T(8,128)} %param.18), kind=kLoop, calls=%fused_computation.17 | loop fusion | flops 4700160 | bytes 6082564 | tf_op jit(solution)/shard_map/convert_element_type | solution.py:493
  331.9 0.0 copy-done.1
  331.9 0.0 copy-done.2
  331.9 0.0 copy-done.3
  331.9 0.0 copy-done.4
  331.9 0.0 copy-done.5
  331.9 0.2 copy-done.6
  332.1 4.3 %fusion.2 = (bf16[2,40,3456]{2,1,0:T(8,128)(2,1)}, f32[2,40,3456]{2,1,0:T(8,128)}, f32[2,40,3456]{2,1,0:T(8,128)}, bf16[2,40,3456]{2,1,0:T(8,128)(2,1)}, f32[2,40,3456]{2,1,0:T(8,128)}, /*index=5*/f32[2,40,3456]{2,1,0:T(8,128)}) fusion(bf16[2,40,3456]{2,1,0:T(8,128)(2,1)S(1)} %copy-done.1, f32[]{:T(128)S(6)} %min_shard_map.3, ...), kind=kLoop, calls=%fused_computation.11 | loop fusion | flops 9400320 | bytes 12165124 | tf_op jit(solution)/shard_map/convert_element_type | solution.py:493
Async XLA Ops:
  0.6 327.4 %copy-start = (bf16[2,216,640]{2,1,0:T(8,128)(2,1)S(1)}, bf16[2,216,640]{2,1,0:T(8,128)(2,1)}, u32[]{:S(2)}) copy-start(bf16[2,216,640]{2,1,0:T(8,128)(2,1)} %wd.1) | copy-start | bytes 1658884
  328.1 3.8 %copy-start.1 = (bf16[2,40,3456]{2,1,0:T(8,128)(2,1)S(1)}, bf16[2,40,3456]{2,1,0:T(8,128)(2,1)}, u32[]{:S(2)}) copy-start(bf16[2,40,3456]{2,1,0:T(8,128)(2,1)} %wg.1) | copy-start | bytes 1658884
  328.1 3.8 %copy-start.2 = (bf16[2,40,3456]{2,1,0:T(8,128)(2,1)S(1)}, bf16[2,40,3456]{2,1,0:T(8,128)(2,1)}, u32[]{:S(2)}) copy-start(bf16[2,40,3456]{2,1,0:T(8,128)(2,1)} %wu.1) | copy-start | bytes 1658884
  328.1 3.8 %copy-start.3 = (f32[2,40,3456]{2,1,0:T(8,128)S(1)}, f32[2,40,3456]{2,1,0:T(8,128)}, u32[]{:S(2)}) copy-start(f32[2,40,3456]{2,1,0:T(8,128)} %param.19) | copy-start | bytes 3317764
  328.1 3.8 %copy-start.4 = (f32[2,40,3456]{2,1,0:T(8,128)S(1)}, f32[2,40,3456]{2,1,0:T(8,128)}, u32[]{:S(2)}) copy-start(f32[2,40,3456]{2,1,0:T(8,128)} %param.16) | copy-start | bytes 3317764
  328.1 3.8 %copy-start.5 = (f32[2,40,3456]{2,1,0:T(8,128)S(1)}, f32[2,40,3456]{2,1,0:T(8,128)}, u32[]{:S(2)}) copy-start(f32[2,40,3456]{2,1,0:T(8,128)} %param.20) | copy-start | bytes 3317764
  328.1 4.0 %copy-start.6 = (f32[2,40,3456]{2,1,0:T(8,128)S(1)}, f32[2,40,3456]{2,1,0:T(8,128)}, u32[]{:S(2)}) copy-start(f32[2,40,3456]{2,1,0:T(8,128)} %param.17) | copy-start | bytes 3317764

commit v2 on v1

--- a/solution.py
+++ b/solution.py
@@ -1,4 +1,5 @@
 import functools
+import math
 
 import jax
 import jax.numpy as jnp
@@ -14,6 +15,7 @@
 SLOTS = 8
 GSLOTS = 16
 RSLOTS = 8
+GPAR = 2
 DCH = 3
 CHUNKS = 9
 PIECES = 9
@@ -31,9 +33,9 @@
     return lax.dot_general(a, b, (((0,), (0,)), ((), ())), preferred_element_type=F32)
 
 
-def train_kernel(nz, x, dy, wg, wu, wd, ggu, gd, sqo, WGU, WD,
+def train_kernel(nz, ny, x, dy, wg, wu, wd, ggu, gd, sqo, WGU, WD,
                  H, DY, A, AT, DACC, WC, WDC, DGU, ACT, TS, R, TD, RD, BG, BD, FG, FD, SQ, SQALL, sgu, sd,
-                 load_sem, w_sem, own_sem, g_recv, g_sib, g_send,
+                 load_sem, w_sem, own_sem, g_recv, g_sib, g_send, g_par,
                  r_send, r_recv, ring_send, ring_recv, fin_send, fin_recv, sq_send, sq_recv):
     me = lax.axis_index("dp")
     z, c = me // 2, me % 2
@@ -52,10 +54,18 @@
     total = 2 * per
     gper = DCH + CHUNKS
     gtotal = 2 * gper
-    gdone = SK * half + 2
+    dhalf = (drow // 16 + 1) * 8
+    gpar = SK * half + GPAR
+    gdone = gpar + 1
     UF = DCH + gdone + 1
     U1 = gper + DCH + gdone + 1
     U2 = U1 + CHUNKS + 1
+
+    rep = lax.axis_index("rep")
+    gx, gy = rep // ny, rep % ny
+    diagonal = lax.rem(gx + gy, 2)
+    beside_y = rep + 1 - 2 * lax.rem(gy, 2)
+    beside_x = rep + ny * (1 - 2 * lax.rem(gx, 2))
 
     def dev(zz, cc):
         return {"dp": lax.rem(zz + nz, nz) * 2 + cc}
@@ -76,7 +86,9 @@
     barrier = pltpu.get_barrier_semaphore()
     for i in range(1, n):
         pl.semaphore_signal(barrier, inc=1, device_id={"dp": lax.rem(me + i, n)}, device_id_type=MESH)
-    pl.semaphore_wait(barrier, n - 1)
+    for to in (beside_x, beside_y):
+        pl.semaphore_signal(barrier, inc=1, device_id={"rep": to, "dp": me}, device_id_type=MESH)
+    pl.semaphore_wait(barrier, n + 1)
     for cp in first:
         cp.wait()
     pltpu.make_async_copy(WGU.at[:, :rgu, :], sgu, load_sem.at[3]).wait()
@@ -94,18 +106,34 @@
             return 0
         lax.fori_loop(0, tokens // 128, rows, 0)
 
-    def piece(q, src_z, own, fn):
+    def piece(q, blk, part, own, fn):
         layer, r = q // gper, q % gper
-        blk = lax.rem(src_z + nz, nz) * 2 + c
         @pl.when(r < DCH)
         def _():
-            dst = WD.at[layer, pl.ds(pl.multiple_of(blk * rd + r * drow, 8), drow), :]
-            fn(sd.at[layer, pl.ds(pl.multiple_of(r * drow, 8), drow), :] if own else dst, dst)
+            def rows(first, size):
+                here = pl.ds(pl.multiple_of(r * drow + first, 8), size)
+                dst = WD.at[layer, pl.ds(pl.multiple_of(blk * rd + r * drow + first, 8), size), :]
+                fn(sd.at[layer, here, :] if own else dst, dst)
+            if part == 2:
+                rows(0, drow)
+            else:
+                @pl.when(diagonal == part)
+                def _():
+                    rows(0, dhalf)
+                @pl.when(diagonal != part)
+                def _():
+                    rows(dhalf, drow - dhalf)
         @pl.when(r >= DCH)
         def _():
-            cs = pl.ds(pl.multiple_of((r - DCH) * 2 * cw, 128), 2 * cw)
+            start, size = (r - DCH) * 2 * cw, 2 * cw
+            if part < 2:
+                start, size = start + lax.rem(diagonal + part, 2) * cw, cw
+            cs = pl.ds(pl.multiple_of(start, 128), size)
             dst = WGU.at[layer, pl.ds(pl.multiple_of(blk * rgu, 8), rgu), cs]
             fn(sgu.at[layer, :, cs] if own else dst, dst)
+
+    def block(zz):
+        return lax.rem(zz + nz, nz) * 2 + c
 
     def to_sibling(q, src, dst):
         remote(src, dst, g_send.at[q % GSLOTS], g_sib.at[q % GSLOTS], dev(z, 1 - c)).start()
@@ -114,15 +142,21 @@
         to = z + 1 if way == 0 else z - 1
         remote(src, dst, g_send.at[q % GSLOTS], g_recv.at[way, hop - 1, q % RSLOTS], dev(to, c)).start()
 
+    def to_beside(q, src, dst):
+        to = jnp.where(q % 2 == 0, beside_y, beside_x)
+        remote(src, dst, g_send.at[q % GSLOTS], g_par.at[q % GSLOTS], {"rep": to, "dp": me}).start()
+
     def gather_step(t):
         @pl.when(t < gtotal)
         def _():
             def own(src, dst):
                 to_next(t, 0, 1, src, dst)
                 to_next(t, 1, 1, src, dst)
+            piece(t, me, 0, True, own)
+            def whole(src, dst):
                 to_sibling(t, src, dst)
                 pltpu.make_async_copy(src, dst, own_sem.at[t % GSLOTS]).start()
-            piece(t, z, True, own)
+            piece(t, me, 2, True, whole)
         for h in range(1, half + 1):
             q = t - SK * h
             for way in (0, 1):
@@ -140,23 +174,44 @@
                             @pl.when(longer)
                             def _():
                                 to_next(q, way, h + 1, src, dst)
+                        to_beside(q, src, dst)
                         to_sibling(q, src, dst)
-                    piece(q, z - h if way == 0 else z + h, False, go)
+                    piece(q, block(z - h if way == 0 else z + h), 0, False, go)
+        q = t - gpar
+        @pl.when((q >= 0) & (q < gtotal))
+        def _():
+            layer, r, slot = q // gper, q % gper, q % GSLOTS
+            @pl.when(r < DCH)
+            def _():
+                for theirs in range(2):
+                    @pl.when(diagonal != theirs)
+                    def _():
+                        wait(WD.at[layer, pl.ds(0, (nz - 1) * (drow - dhalf if theirs else dhalf)), :], g_par.at[slot])
+            @pl.when(r >= DCH)
+            def _():
+                wait(WGU.at[layer, pl.ds(0, (nz - 1) * rgu), pl.ds(0, cw)], g_par.at[slot])
+            for h in range(1, nz):
+                piece(q, block(z + h), 1, False, lambda src, dst: to_sibling(q, src, dst))
         q = t - gdone
         @pl.when((q >= 0) & (q < gtotal))
         def _():
             layer, r, slot = q // gper, q % gper, q % GSLOTS
-            def both(ref):
-                for rows, sem in ((1, own_sem), (nz, g_sib), (2 * nz - 1, g_send)):
-                    a = ref(rows)
-                    pltpu.make_async_copy(a, a, sem.at[slot]).wait()
+            def waited(ref, sem):
+                pltpu.make_async_copy(ref, ref, sem.at[slot]).wait()
             @pl.when(r < DCH)
             def _():
-                both(lambda k: WD.at[layer, pl.ds(0, k * drow), :])
+                rows = lambda k: WD.at[layer, pl.ds(0, k), :]
+                waited(rows(drow), own_sem)
+                waited(rows(nz * drow), g_sib)
+                for mine in range(2):
+                    @pl.when(diagonal == mine)
+                    def _():
+                        waited(rows(nz * drow + 2 * (nz - 1) * (drow - dhalf if mine else dhalf)), g_send)
             @pl.when(r >= DCH)
             def _():
                 cs = pl.ds(pl.multiple_of((r - DCH) * 2 * cw, 128), 2 * cw)
-                both(lambda k: WGU.at[layer, pl.ds(0, k * rgu), cs])
+                for k, sem in ((1, own_sem), (nz, g_sib), (2 * nz - 1, g_send)):
+                    waited(WGU.at[layer, pl.ds(0, k * rgu), cs], sem)
 
     def work(u):
         k0, k1, k2 = u - UF, u - U1, u - U2
@@ -464,7 +519,7 @@
     V, S = pltpu.VMEM, pltpu.SemaphoreType.DMA
     shape = jax.ShapeDtypeStruct
     return pl.pallas_call(
-        functools.partial(train_kernel, nz),
+        functools.partial(train_kernel, nz, math.isqrt(mesh.shape["rep"])),
         out_shape=(
             shape((layers, 2, rgu, ff), BF16), shape((layers, rd, d), BF16), shape((8, 128), F32),
             shape((layers, d, 2 * ff), BF16), shape((layers, ff, d), BF16),
@@ -478,7 +533,7 @@
             V((2, half + 1, SLOTS, 2 * rgu, cw), BF16), V((2, half + 1, SLOTS, prow, d), BF16),
             V((SLOTS, 2, rgu, cw), BF16), V((SLOTS, 2, prow // 2, d), BF16),
             V((8, 128), F32), V((n, 8, 128), F32), V((layers, rgu, 2 * ff), BF16), V((layers, rd, d), BF16),
-            S((4,)), S((2, 2)), S((GSLOTS,)), S((2, half, RSLOTS)), S((GSLOTS,)), S((GSLOTS,)),
+            S((4,)), S((2, 2)), S((GSLOTS,)), S((2, half, RSLOTS)), S((GSLOTS,)), S((GSLOTS,)), S((GSLOTS,)),
             S, S((total,)), S((2, half, SLOTS)), S((2, half, SLOTS)), S((2, SLOTS)), S((layers, 2)), S, S,
         ],
         compiler_params=pltpu.CompilerParams(collective_id=0, has_side_effects=True, vmem_limit_bytes=63 * 2**20),

time: 337 us -> 302 us (0.90)
  Pallas kernels: 325 us -> 290 us
    pallas_call x1, Pallas kernels: 325 us -> 290 us  [train(): pl.pallas_call(functools.partial(train_kernel, nz, math.isqrt(mesh.shape[...]
where the time goes in v2:
time: 302 us
  Pallas kernels  290 us (96%)
  other arithmetic  9.37 us (3%)
    pallas_call x1, Pallas kernels, train(): pl.pallas_call(functools.partial(train_kernel, nz, math.isqrt(mesh.shape[...  290 us
    convert_element_type x2, other arithmetic, adamw(): return ((w - 0.02 * step).astype(BF16), m, v)  8.08 us

profile of v2, /device:TPU:21, one launch (start us, length us, event | category | flops | bytes accessed | tf_op | source)
XLA Modules:
  0.0 301.5 jit_solution(16361870983768724872)
XLA Ops:
  0.6 0.0 copy-start
  0.7 290.5 %train.1 = (bf16[2,2,40,3456]{3,2,1,0:T(8,128)(2,1)}, bf16[2,216,640]{2,1,0:T(8,128)(2,1)}, f32[8,128]{1,0:T(8,128)}, bf16[2,640,6912]{2,1,0:T(8,128)(2,1)}, bf16[2,3456,640]{2,1,0:T(8,128)(2,1)}) custom-call(bf16[1024,640]{1,0:T(8,128)(2,1)} %bitcast.24, bf16[1024,640]{1,0:T(8,128)(2,1)} %bitcast.25, bf16[2,40,3456]{2,1,0:T(8,128)(2,1)} %wg.1, ...), custom_call_target="tpu_custom_call" | custom-call | tf_op jit(solution)/shard_map/train/pallas_call | solution.py:521
  291.1 1.3 reduce_sum.9
  293.1 0.0 copy-done
  293.1 0.0 copy-start.1
  293.1 0.0 copy-start.2
  293.1 0.0 copy-start.3
  293.2 0.0 copy-start.4
  293.2 0.0 copy-start.5
  293.2 0.0 copy-start.6
  293.2 3.7 %fusion.8 = (bf16[2,216,640]{2,1,0:T(8,128)(2,1)}, f32[2,216,640]{2,1,0:T(8,128)}, f32[2,216,640]{2,1,0:T(8,128)}) fusion(bf16[2,216,640]{2,1,0:T(8,128)(2,1)S(1)} %copy-done, f32[]{:T(128)S(6)} %min_shard_map.3, bf16[2,216,640]{2,1,0:T(8,128)(2,1)} %get-tuple-element.14, f32[2,216,640]{2,1,0:T(8,128)} %param.21, f32[2,216,640]{2,1,0:T(8,128)} %param.18), kind=kLoop, calls=%fused_computation.17 | loop fusion | flops 4700160 | bytes 6082564 | tf_op jit(solution)/shard_map/convert_element_type | solution.py:548
  296.9 0.0 copy-done.1
  296.9 0.0 copy-done.2
  296.9 0.0 copy-done.3
  297.0 0.0 copy-done.4
  297.0 0.0 copy-done.5
  297.0 0.2 copy-done.6
  297.2 4.3 %fusion.2 = (bf16[2,40,3456]{2,1,0:T(8,128)(2,1)}, f32[2,40,3456]{2,1,0:T(8,128)}, f32[2,40,3456]{2,1,0:T(8,128)}, bf16[2,40,3456]{2,1,0:T(8,128)(2,1)}, f32[2,40,3456]{2,1,0:T(8,128)}, /*index=5*/f32[2,40,3456]{2,1,0:T(8,128)}) fusion(bf16[2,40,3456]{2,1,0:T(8,128)(2,1)S(1)} %copy-done.1, f32[]{:T(128)S(6)} %min_shard_map.3, ...), kind=kLoop, calls=%fused_computation.11 | loop fusion | flops 9400320 | bytes 12165124 | tf_op jit(solution)/shard_map/convert_element_type | solution.py:548
Async XLA Ops:
  0.6 292.5 %copy-start = (bf16[2,216,640]{2,1,0:T(8,128)(2,1)S(1)}, bf16[2,216,640]{2,1,0:T(8,128)(2,1)}, u32[]{:S(2)}) copy-start(bf16[2,216,640]{2,1,0:T(8,128)(2,1)} %wd.1) | copy-start | bytes 1658884
  293.1 3.8 %copy-start.1 = (bf16[2,40,3456]{2,1,0:T(8,128)(2,1)S(1)}, bf16[2,40,3456]{2,1,0:T(8,128)(2,1)}, u32[]{:S(2)}) copy-start(bf16[2,40,3456]{2,1,0:T(8,128)(2,1)} %wg.1) | copy-start | bytes 1658884
  293.1 3.8 %copy-start.2 = (bf16[2,40,3456]{2,1,0:T(8,128)(2,1)S(1)}, bf16[2,40,3456]{2,1,0:T(8,128)(2,1)}, u32[]{:S(2)}) copy-start(bf16[2,40,3456]{2,1,0:T(8,128)(2,1)} %wu.1) | copy-start | bytes 1658884
  293.1 3.8 %copy-start.3 = (f32[2,40,3456]{2,1,0:T(8,128)S(1)}, f32[2,40,3456]{2,1,0:T(8,128)}, u32[]{:S(2)}) copy-start(f32[2,40,3456]{2,1,0:T(8,128)} %param.19) | copy-start | bytes 3317764
  293.2 3.8 %copy-start.4 = (f32[2,40,3456]{2,1,0:T(8,128)S(1)}, f32[2,40,3456]{2,1,0:T(8,128)}, u32[]{:S(2)}) copy-start(f32[2,40,3456]{2,1,0:T(8,128)} %param.16) | copy-start | bytes 3317764
  293.2 3.8 %copy-start.5 = (f32[2,40,3456]{2,1,0:T(8,128)S(1)}, f32[2,40,3456]{2,1,0:T(8,128)}, u32[]{:S(2)}) copy-start(f32[2,40,3456]{2,1,0:T(8,128)} %param.20) | copy-start | bytes 3317764
  293.2 4.0 %copy-start.6 = (f32[2,40,3456]{2,1,0:T(8,128)S(1)}, f32[2,40,3456]{2,1,0:T(8,128)}, u32[]{:S(2)}) copy-start(f32[2,40,3456]{2,1,0:T(8,128)} %param.17) | copy-start | bytes 3317764

commit v3 on v2

v3 whole, which is shorter than its diff:
```python
import functools
import math

import jax
import jax.numpy as jnp
from jax import lax
from jax.experimental import pallas as pl
from jax.experimental.pallas import tpu as pltpu
from jax.sharding import PartitionSpec as P

MESH = pl.DeviceIdType.MESH
ANY = pl.BlockSpec(memory_space=pltpu.HBM)
F32, BF16 = jnp.float32, jnp.bfloat16
SK = 2
SLOTS = 8
GSLOTS = 16
RSLOTS = 8
GPAR = 2
GDONE = 2
GSK = 2
DCH = 3
CHUNKS = 9
SPREAD = 1
THREE = 3
PIECES = 9


def mm(a, b):
    return jnp.dot(a, b, preferred_element_type=F32)


def mm_nt(a, b):
    return lax.dot_general(a, b, (((1,), (1,)), ((), ())), preferred_element_type=F32)


def mm_tn(a, b):
    return lax.dot_general(a, b, (((0,), (0,)), ((), ())), preferred_element_type=F32)


def train_kernel(nz, ny, x, dy, wg, wu, wd, ggu, gd, sqo, WGU, WD, GUH, DGH, AH, ATH,
                 H, DY, A, AT, DACC, WC, WDC, GUS, DGU, ACT, TS, R, TD, RD, BG, BD, FG, FD, SQ, SQALL, sgu, sd,
                 load_sem, w_sem, gu_sem, dg_sem, own_sem, g_recv, g_sib, g_send, g_par,
                 r_send, r_recv, rd_send, rd_recv, ring_send, ring_recv, dring_send, dring_recv, fin_send, dfin_send, fin_recv, sq_send, sq_recv):
    me = lax.axis_index("dp")
    z, c = me // 2, me % 2
    n = 2 * nz
    half = nz // 2
    tokens, d = H.shape
    rgu = d // n
    cw = TS.shape[-1]
    ff = cw * CHUNKS
    rd = ff // n
    drow = rd // DCH
    crd = 2 * rd
    prow = crd // PIECES
    items = (PIECES + 1) // 2
    gper = DCH + CHUNKS
    gtotal = 2 * gper
    dhalf = (drow // 16 + 1) * 8
    gpar = GSK * half + GPAR
    gdone = gpar + GDONE
    UF = DCH + gdone + 1
    U1 = UF + CHUNKS
    UB = U1 + CHUNKS
    UC = UB + CHUNKS // THREE + 1
    G1, G0, D1, D0 = 1, UC - U1 + 1, CHUNKS + 1, UC - U1 + CHUNKS + 1

    def gathered(u):
        return jnp.where(u < UF, u, UF + lax.div(4 * (u - UF), 3))

    rep = lax.axis_index("rep")
    gx, gy = rep // ny, rep % ny
    diagonal = lax.rem(gx + gy, 2)
    beside_y = rep + 1 - 2 * lax.rem(gy, 2)
    beside_x = rep + ny * (1 - 2 * lax.rem(gx, 2))

    def dev(zz, cc):
        return {"dp": lax.rem(zz + nz, nz) * 2 + cc}

    up, down, sibling = dev(z + 1, c), dev(z - 1, c), dev(z, 1 - c)

    def remote(src, dst, s, r, to):
        return pltpu.make_async_remote_copy(src, dst, s, r, device_id=to, device_id_type=MESH)

    def wait(ref, sem):
        remote(ref, ref, sem, sem, sibling).wait_recv()

    first = [pltpu.make_async_copy(x, H, load_sem.at[0]), pltpu.make_async_copy(dy, DY, load_sem.at[1]), pltpu.make_async_copy(wd, sd, load_sem.at[2])]
    for cp in first:
        cp.start()
    for j in range(CHUNKS):
        for m, w in enumerate((wg, wu)):
            pltpu.make_async_copy(w.at[:, :, j * cw : (j + 1) * cw], sgu.at[:, j, m], load_sem.at[3]).start()

    barrier = pltpu.get_barrier_semaphore()
    for i in range(1, n):
        pl.semaphore_signal(barrier, inc=1, device_id={"dp": lax.rem(me + i, n)}, device_id_type=MESH)
    for to in (beside_x, beside_y):
        pl.semaphore_signal(barrier, inc=1, device_id={"rep": to, "dp": me}, device_id_type=MESH)
    pl.semaphore_wait(barrier, n + 1)
    for cp in first:
        cp.wait()
    pltpu.make_async_copy(WGU.at[:, :, :, :rgu, :], sgu, load_sem.at[3]).wait()

    SQ[...] = jnp.zeros_like(SQ)

    def normalize(src, transposed):
        def rows(i, _):
            rs = pl.ds(pl.multiple_of(i * 128, 128), 128)
            wide = src[rs, :].astype(F32)
            a = (wide * lax.rsqrt(jnp.mean(wide * wide, -1, keepdims=True) + 1e-6)).astype(BF16)
            A[rs, :] = a
            if transposed:
                AT[:, rs] = a.T
            return 0
        lax.fori_loop(0, tokens // 128, rows, 0)

    def chunk(q):
        layer = jnp.where(q >= gper, 1, 0)
        r = q - layer * gper
        return layer, r < DCH, jnp.where(r < DCH, r, r - DCH)

    def piece(q, blk, part, own, fn):
        layer, is_down, r = chunk(q)
        @pl.when(is_down)
        def _():
            def rows(first, size):
                here = pl.ds(pl.multiple_of(r * drow + first, 8), size)
                dst = WD.at[layer, pl.ds(pl.multiple_of(blk * rd + r * drow + first, 8), size), :]
                fn(sd.at[layer, here, :] if own else dst, dst)
            if part == 2:
                rows(0, drow)
            else:
                @pl.when(diagonal == part)
                def _():
                    rows(0, dhalf)
                @pl.when(diagonal != part)
                def _():
                    rows(dhalf, drow - dhalf)
        @pl.when(jnp.logical_not(is_down))
        def _():
            which = pl.ds(0, 2) if part == 2 else lax.rem(diagonal + part, 2)
            dst = WGU.at[layer, r, which, pl.ds(pl.multiple_of(blk * rgu, 8), rgu), :]
            fn(sgu.at[layer, r, which] if own else dst, dst)

    def block(zz):
        return jnp.where(zz >= nz, zz - nz, jnp.where(zz < 0, zz + nz, zz)) * 2 + c

    def to_sibling(q, src, dst):
        remote(src, dst, g_send.at[lax.rem(q, GSLOTS)], g_sib.at[lax.rem(q, GSLOTS)], sibling).start()

    def to_next(q, way, hop, src, dst):
        remote(src, dst, g_send.at[lax.rem(q, GSLOTS)], g_recv.at[way, hop - 1, lax.rem(q, RSLOTS)], (up, down)[way]).start()

    def to_beside(q, src, dst):
        to = jnp.where(lax.rem(q, 2) == 0, beside_y, beside_x)
        remote(src, dst, g_send.at[lax.rem(q, GSLOTS)], g_par.at[lax.rem(q, GSLOTS)], {"rep": to, "dp": me}).start()

    def gather_step(t):
        @pl.when(t < gtotal)
        def _():
            def own(src, dst):
                to_next(t, 0, 1, src, dst)
                to_next(t, 1, 1, src, dst)
            piece(t, me, 0, True, own)
            def whole(src, dst):
                to_sibling(t, src, dst)
                pltpu.make_async_copy(src, dst, own_sem.at[lax.rem(t, GSLOTS)]).start()
            piece(t, me, 2, True, whole)
        for h in range(1, half + 1):
            q = t - GSK * h
            for way in (0, 1):
                longer = lax.rem(q, 2) == way
                ok = (q >= 0) & (q < gtotal)
                if h == half:
                    ok = ok & longer
                @pl.when(ok)
                def _():
                    def go(src, dst):
                        remote(src, dst, g_send.at[0], g_recv.at[way, h - 1, lax.rem(q, RSLOTS)], sibling).wait_recv()
                        if h < half - 1:
                            to_next(q, way, h + 1, src, dst)
                        elif h == half - 1:
                            @pl.when(longer)
                            def _():
                                to_next(q, way, h + 1, src, dst)
                        to_beside(q, src, dst)
                    piece(q, block(z - h if way == 0 else z + h), 0, False, go)
        q = t - gpar
        @pl.when((q >= 0) & (q < gtotal))
        def _():
            layer, is_down, r = chunk(q)
            slot = lax.rem(q, GSLOTS)
            @pl.when(is_down)
            def _():
                for theirs in range(2):
                    @pl.when(diagonal != theirs)
                    def _():
                        wait(WD.at[layer, pl.ds(0, (nz - 1) * (drow - dhalf if theirs else dhalf)), :], g_par.at[slot])
            @pl.when(jnp.logical_not(is_down))
            def _():
                wait(WGU.at[layer, 0, 0, pl.ds(0, (nz - 1) * rgu), :], g_par.at[slot])
            for h in range(1, nz):
                piece(q, block(z + h), 2, False, lambda src, dst: to_sibling(q, src, dst))
        q = t - gdone
        @pl.when((q >= 0) & (q < gtotal))
        def _():
            layer, is_down, r = chunk(q)
            slot = lax.rem(q, GSLOTS)
            def waited(ref, sem):
                pltpu.make_async_copy(ref, ref, sem.at[slot]).wait()
            @pl.when(is_down)
            def _():
                rows = lambda k: WD.at[layer, pl.ds(0, k), :]
                waited(rows(drow), own_sem)
                waited(rows(nz * drow), g_sib)
                for mine in range(2):
                    @pl.when(diagonal == mine)
                    def _():
                        waited(rows(nz * drow + 2 * (nz - 1) * (drow - dhalf if mine else dhalf)), g_send)
            @pl.when(jnp.logical_not(is_down))
            def _():
                for k, sem in ((1, own_sem), (nz, g_sib), (2 * nz - 1, g_send)):
                    waited(WGU.at[layer, 0, :, pl.ds(0, k * rgu), :], sem)

    def work(u):
        ks = [u - first for first in (UF, U1, UB, UC)]
        on = functools.reduce(jnp.logical_or, [(k >= 0) & (k < (CHUNKS // THREE if first == UB else CHUNKS)) for k, first in zip(ks, (UF, U1, UB, UC))])
        pick = lambda a, b, c, d: jnp.where(u < U1, a, jnp.where(u < UB, b, jnp.where(u < UC, c, d)))
        return on, pick(0, 1, 2, 3), pick(*ks)

    def loads(u):
        on, kind, j = work(u)
        layer = jnp.where((kind == 0) | (kind == 3), 0, 1)
        slot = lax.rem(u, 2)
        return (
            (on & (kind < 2), pltpu.make_async_copy(WGU.at[layer, j, 0], WC.at[slot, :, pl.ds(0, cw)], w_sem.at[slot, 0])),
            (on & (kind < 2), pltpu.make_async_copy(WGU.at[layer, j, 1], WC.at[slot, :, pl.ds(cw, cw)], w_sem.at[slot, 1])),
            (on & (kind != 2), pltpu.make_async_copy(WD.at[layer, pl.ds(pl.multiple_of(j * cw, 128), cw), :], WDC.at[slot], w_sem.at[slot, 2])),
            (on & (kind == 3), pltpu.make_async_copy(GUH.at[j], GUS.at[slot], w_sem.at[slot, 4])),
        )

    def kept(j, slot, buf, hbm, sem):
        return pltpu.make_async_copy(buf.at[slot], hbm.at[j], sem.at[slot])

    def forward(j, slot):
        @pl.when(j >= 2)
        def _():
            kept(j, slot, GUS, GUH, gu_sem).wait()
        gu = mm(A[...], WC[slot])
        GUS[slot] = gu
        kept(j, slot, GUS, GUH, gu_sem).start()
        g, up = gu[:, :cw], gu[:, cw:]
        ACT[...] = (g * jax.nn.sigmoid(g) * up).astype(BF16)
        @pl.when(j == 0)
        def _():
            DACC[...] = jnp.zeros_like(DACC)
        DACC[...] += mm(ACT[...], WDC[slot])

    def down_gradient(layer, j):
        TD[layer, pl.ds(pl.multiple_of(j * cw, 128), cw), :] = mm_tn(ACT[...], DY[...]).astype(BF16)

    def backward(gu, j, slot):
        g, up = gu[:, :cw], gu[:, cw:]
        back = mm_nt(DY[...], WDC[slot]).astype(BF16).astype(F32)
        sg = jax.nn.sigmoid(g)
        s = g * sg
        ACT[...] = (s * up).astype(BF16)
        DGU[slot, :, :cw] = (back * up * (sg + s * (1.0 - sg))).astype(BF16)
        DGU[slot, :, cw:] = (back * s).astype(BF16)
        t = mm(AT[...], DGU[slot]).astype(BF16)
        TS[0, j] = t[:, :cw]
        TS[1, j] = t[:, cw:]

    def second_layer(j, slot):
        @pl.when(j >= 2)
        def _():
            kept(j, slot, DGU, DGH, dg_sem).wait()
        backward(mm(A[...], WC[slot]), j, slot)
        @pl.when(j < CHUNKS - 2)
        def _():
            kept(j, slot, DGU, DGH, dg_sem).start()

    def first_layer(j, slot):
        backward(GUS[slot], j, slot)

    def input_gradient(step):
        def again(k, slot):
            return (pltpu.make_async_copy(WGU.at[1, k, 0], WC.at[slot, :, pl.ds(0, cw)], w_sem.at[slot, 0]),
                    pltpu.make_async_copy(WGU.at[1, k, 1], WC.at[slot, :, pl.ds(cw, cw)], w_sem.at[slot, 1]),
                    pltpu.make_async_copy(DGH.at[k], DGU.at[slot], w_sem.at[slot, 3]))

        def one(i, _):
            m = THREE * step + i
            slot = lax.rem(m + U1 + CHUNKS, 2)
            @pl.when(m >= 2)
            def _():
                for copy in again(CHUNKS - 1 - m, slot):
                    copy.wait()
            @pl.when(m == 0)
            def _():
                DACC[...] = jnp.zeros_like(DACC)
            DACC[...] += mm_nt(DGU[slot], WC[slot])
            @pl.when(m + 2 < CHUNKS)
            def _():
                for copy in again(CHUNKS - 3 - m, slot):
                    copy.start()
            return 0
        lax.fori_loop(0, THREE, one, 0)

    def after_forward():
        def rows(i, _):
            rs = pl.ds(pl.multiple_of(i * 128, 128), 128)
            H[rs, :] = (H[rs, :].astype(F32) + DACC[rs, :].astype(BF16).astype(F32)).astype(BF16)
            return 0
        lax.fori_loop(0, tokens // 128, rows, 0)
        normalize(H, True)

    def between():
        def rows(i, _):
            rs = pl.ds(pl.multiple_of(i * 128, 128), 128)
            wide = H[rs, :].astype(F32)
            scale = lax.rsqrt(jnp.mean(wide * wide, -1, keepdims=True) + 1e-6)
            da = DACC[rs, :].astype(BF16).astype(F32)
            dh = scale * da - wide * (scale * scale * scale * jnp.mean(wide * da, -1, keepdims=True))
            DY[rs, :] = (DY[rs, :].astype(F32) + dh.astype(BF16).astype(F32)).astype(BF16)
            return 0
        lax.fori_loop(0, tokens // 128, rows, 0)

    class Item:
        pass

    def gu_item(t, s):
        e = Item()
        i = t - G1 - SK * s
        second = i < CHUNKS
        e.r = jnp.where(second, i, i - (G0 - G1))
        e.valid = (e.r >= 0) & (e.r < CHUNKS)
        e.layer = jnp.where(second, 1, 0)
        e.i, e.slot, e.odd, e.gu = i, lax.rem(i, SLOTS), lax.rem(e.r, 2), True
        e.buf, e.sent, e.come = BG, ring_send, ring_recv
        return e

    def d_item(t, s, layer):
        e = Item()
        if layer == 1:
            i = t - D1 - SK * s
            e.valid = (i >= 0) & (i < SPREAD * items) & (lax.rem(i, SPREAD) == 0)
            k = lax.div(i, SPREAD)
        else:
            k = t - D0 - s
            e.valid = (k >= 0) & (k < items)
        e.p = 2 * k + (1 - c if layer == 1 else c)
        e.valid = e.valid & (e.p < PIECES)
        e.k, e.layer, e.odd, e.gu = k, layer, lax.rem(k, 2), False
        e.slot = k
        e.buf, e.sent, e.come = BD, dring_send, dring_recv
        return e

    def terms(e, zz):
        if e.gu:
            rs = pl.ds(pl.multiple_of(zz * (2 * rgu), 16), 2 * rgu)
            return TS[c, e.r, rs, :].astype(F32) + R[e.r, rs, :].astype(F32)
        rs = pl.ds(pl.multiple_of(zz * crd + e.p * prow, 16), prow)
        return TD[e.layer, rs, :].astype(F32) + RD[e.slot, zz].astype(F32)

    def around(zz):
        return jnp.where(zz >= nz, zz - nz, jnp.where(zz < 0, zz + nz, zz))

    def ring_copy(e, way, s):
        return remote(e.buf.at[way, s, e.slot], e.buf.at[way, s + 1, e.slot], e.sent.at[way, s, e.slot], e.come.at[way, s, e.slot], (up, down)[way])

    def stage(e, s):
        def go(way):
            far = half - 1 - s + jnp.where(e.odd == way, 1, 0)
            t = terms(e, around(z + far if way == 0 else z - far))
            if s > 0:
                wait(e.buf.at[way, s, e.slot], e.come.at[way, s - 1, e.slot])
                t = t + e.buf[way, s, e.slot].astype(F32)
            e.buf[way, s, e.slot] = t.astype(BF16)
            ring_copy(e, way, s).start()
        if s < half - 1:
            @pl.when(e.valid)
            def _():
                go(0)
                go(1)
        else:
            for way in (0, 1):
                @pl.when(e.valid & (e.odd == way))
                def _():
                    go(way)

    def stage_sent(e, s):
        if s < half - 1:
            @pl.when(e.valid)
            def _():
                ring_copy(e, 0, s).wait_send()
                ring_copy(e, 1, s).wait_send()
        else:
            for way in (0, 1):
                @pl.when(e.valid & (e.odd == way))
                def _():
                    ring_copy(e, way, s).wait_send()

    def last(e):
        @pl.when(e.valid)
        def _():
            t = terms(e, z)
            for way in (0, 1):
                hops = half - 1 + jnp.where(e.odd == way, 1, 0)
                wait(e.buf.at[way, hops, e.slot], e.come.at[way, hops - 1, e.slot])
                t = t + e.buf[way, hops, e.slot].astype(F32)
            w = t.astype(BF16).astype(F32)
            sq = SQ[...]
            for a in range(w.shape[0] // 8):
                for b in range(w.shape[1] // 128):
                    v = w[8 * a : 8 * a + 8, 128 * b : 128 * b + 128]
                    sq = sq + v * v
            SQ[...] = sq
            out, rows = (FG, rgu) if e.gu else (FD, prow // 2)
            out[e.slot, 0] = w[:rows].astype(BF16)
            out[e.slot, 1] = w[rows:].astype(BF16)
            if e.gu:
                cs = pl.ds(pl.multiple_of(e.r * cw, 128), cw)
                pltpu.make_async_copy(FG.at[e.slot, c], ggu.at[e.layer, c, :, cs], fin_send.at[0, e.slot]).start()
                remote(FG.at[e.slot, 1 - c], ggu.at[e.layer, c, :, cs], fin_send.at[1, e.slot], fin_recv.at[e.layer, 0], sibling).start()
            else:
                for b in range(2):
                    k = 2 * e.p + b
                    theirs = k >= PIECES
                    row = jnp.where(theirs, k - PIECES, k) * (prow // 2)
                    dst = gd.at[e.layer, pl.ds(pl.multiple_of(row, 8), prow // 2), :]
                    owner = jnp.where(theirs, 1, 0)
                    @pl.when(owner == c)
                    def _():
                        pltpu.make_async_copy(FD.at[e.slot, b], dst, dfin_send.at[b, e.slot]).start()
                    @pl.when(owner != c)
                    def _():
                        remote(FD.at[e.slot, b], dst, dfin_send.at[b, e.slot], fin_recv.at[e.layer, 1], sibling).start()

    def last_sent(e):
        @pl.when(e.valid)
        def _():
            for b in range(2):
                if e.gu:
                    wait(FG.at[e.slot, b], fin_send.at[b, e.slot])
                else:
                    wait(FD.at[e.slot, b], dfin_send.at[b, e.slot])

    streams = (gu_item, lambda t, s: d_item(t, s, 1), lambda t, s: d_item(t, s, 0))

    def send_terms(t):
        e = gu_item(t + 1, 0)
        @pl.when(e.valid)
        def _():
            remote(TS.at[1 - c, e.r], R.at[e.r], r_send, r_recv.at[e.r], sibling).start()
        for layer in (1, 0):
            e = d_item(t + 1, 0, layer)
            p = 2 * e.k + (c if layer == 1 else 1 - c)
            there = d_valid(t + 1, layer) & (p < PIECES)
            @pl.when(there)
            def _():
                for zz in range(nz):
                    rs = pl.ds(pl.multiple_of(zz * crd + p * prow, 16), prow)
                    remote(TD.at[layer, rs, :], RD.at[e.slot, zz], rd_send, rd_recv.at[e.slot], sibling).start()

    def d_valid(t, layer):
        if layer == 1:
            i = t - D1
            return (i >= 0) & (i < SPREAD * items) & (lax.rem(i, SPREAD) == 0)
        return (t >= D0) & (t < D0 + items)

    def terms_sent(t):
        e = gu_item(t + 1, 0)
        @pl.when(e.valid)
        def _():
            wait(R.at[e.r], r_send)
        for layer in (1, 0):
            e = d_item(t + 1, 0, layer)
            p = 2 * e.k + (c if layer == 1 else 1 - c)
            @pl.when(d_valid(t + 1, layer) & (p < PIECES))
            def _():
                wait(RD.at[e.slot], rd_send)

    def reduce_step(t):
        terms_sent(t - 1)
        for which in streams:
            for s in range(half):
                stage_sent(which(t - 1, s), s)
            last_sent(which(t - 1, half))
        for some in (streams[:2], streams[2:]):
            for which in some:
                last(which(t, half))
            for s in reversed(range(half)):
                for which in some:
                    e = which(t, s)
                    if s == 0:
                        @pl.when(e.valid)
                        def _():
                            if e.gu:
                                wait(R.at[e.r], r_recv.at[e.r])
                            else:
                                wait(RD.at[e.slot], rd_recv.at[e.slot])
                    stage(e, s)

    normalize(H, True)
    keep = (pltpu.make_async_copy(A, AH, load_sem.at[0]), pltpu.make_async_copy(AT, ATH, load_sem.at[1]))
    back = (pltpu.make_async_copy(AH, A, load_sem.at[0]), pltpu.make_async_copy(ATH, AT, load_sem.at[1]))
    for copy in keep:
        copy.start()

    def step(u, _):
        t = u - U1
        @pl.when(gathered(u) < gtotal + gdone)
        def _():
            def one(tg, _):
                gather_step(tg)
                return 0
            lax.fori_loop(gathered(u), gathered(u + 1), one, 0)
        @pl.when(t >= 0)
        def _():
            reduce_step(t)

        on, kind, j = work(u)
        slot = lax.rem(u, 2)
        @pl.when((u == UF + CHUNKS) | (u == UF + CHUNKS + 1))
        def _():
            kept(0, slot, GUS, GUH, gu_sem).wait()
        for there, copy in loads(u + 1):
            @pl.when(there)
            def _():
                copy.start()
        @pl.when(u == U1)
        def _():
            for copy in keep:
                copy.wait()
            after_forward()
        @pl.when(u == UB)
        def _():
            for copy in back:
                copy.start()
        @pl.when(u == UC - 1)
        def _():
            between()
            for copy in back:
                copy.wait()
        for there, copy in loads(u):
            @pl.when(there)
            def _():
                copy.wait()
        @pl.when(on & (kind == 0))
        def _():
            forward(j, slot)
        @pl.when(on & (kind == 1))
        def _():
            second_layer(j, slot)
        @pl.when(on & (kind == 3))
        def _():
            first_layer(j, slot)
        @pl.when(t >= 0)
        def _():
            send_terms(t)
        @pl.when(on & (kind == 1))
        def _():
            down_gradient(1, j)
        @pl.when(on & (kind == 2))
        def _():
            input_gradient(j)
        @pl.when(on & (kind == 3))
        def _():
            down_gradient(0, j)
        return 0

    lax.fori_loop(0, U1 + D0 + items + half + 1, step, 0)

    for i in range(1, n):
        remote(SQ, SQALL.at[me], sq_send, sq_recv, {"dp": lax.rem(me + i, n)}).start()
    for layer in range(2):
        wait(ggu.at[layer, 0], fin_recv.at[layer, 0])
        even = lax.rem(c + layer, 2) == 0
        @pl.when(even)
        def _():
            wait(gd.at[layer, pl.ds(0, PIECES // 2 * (prow // 2)), :], fin_recv.at[layer, 1])
        @pl.when(jnp.logical_not(even))
        def _():
            wait(gd.at[layer, pl.ds(0, (PIECES + 1) // 2 * (prow // 2)), :], fin_recv.at[layer, 1])
    wait(SQALL.at[pl.ds(0, n - 1)], sq_recv)
    acc = SQ[...]
    for i in range(1, n):
        acc = acc + SQALL[lax.rem(me + i, n)]
    sqo[...] = jnp.full((8, 128), jnp.sum(acc), F32)
    wait(SQALL.at[pl.ds(0, n - 1)], sq_send)


def train(mesh, x, dy, w_gate, w_up, w_down):
    n = mesh.shape["dp"]
    nz = n // 2
    half = nz // 2
    tokens, d = x.shape
    layers, rgu, ff = w_gate.shape
    rd = ff // n
    cw = ff // CHUNKS
    prow = 2 * rd // PIECES
    items = (PIECES + 1) // 2
    V, S = pltpu.VMEM, pltpu.SemaphoreType.DMA
    shape = jax.ShapeDtypeStruct
    return pl.pallas_call(
        functools.partial(train_kernel, nz, math.isqrt(mesh.shape["rep"])),
        out_shape=(
            shape((layers, 2, rgu, ff), BF16), shape((layers, rd, d), BF16), shape((8, 128), F32),
            shape((layers, CHUNKS, 2, d, cw), BF16), shape((layers, ff, d), BF16),
            shape((CHUNKS, tokens, 2 * cw), F32), shape((CHUNKS, tokens, 2 * cw), BF16),
            shape((tokens, d), BF16), shape((d, tokens), BF16),
        ),
        in_specs=[ANY] * 5,
        out_specs=(ANY, ANY, pl.BlockSpec(memory_space=pltpu.VMEM), ANY, ANY, ANY, ANY, ANY, ANY),
        scratch_shapes=[
            V((tokens, d), BF16), V((tokens, d), BF16), V((tokens, d), BF16), V((d, tokens), BF16), V((tokens, d), F32),
            V((2, d, 2 * cw), BF16), V((2, cw, d), BF16), V((2, tokens, 2 * cw), F32), V((2, tokens, 2 * cw), BF16), V((tokens, cw), BF16),
            V((2, CHUNKS, d, cw), BF16), V((CHUNKS, d, cw), BF16), V((layers, ff, d), BF16), V((items, nz, prow, d), BF16),
            V((2, half + 1, SLOTS, 2 * rgu, cw), BF16), V((2, half + 1, items, prow, d), BF16),
            V((SLOTS, 2, rgu, cw), BF16), V((items, 2, prow // 2, d), BF16),
            V((8, 128), F32), V((n, 8, 128), F32), V((layers, CHUNKS, 2, rgu, cw), BF16), V((layers, rd, d), BF16),
            S((4,)), S((2, 5)), S((2,)), S((2,)), S((GSLOTS,)), S((2, half, RSLOTS)), S((GSLOTS,)), S((GSLOTS,)), S((GSLOTS,)),
            S, S((CHUNKS,)), S, S((items,)), S((2, half, SLOTS)), S((2, half, SLOTS)), S((2, half, items)), S((2, half, items)),
            S((2, SLOTS)), S((2, items)), S((layers, 2)), S, S,
        ],
        compiler_params=pltpu.CompilerParams(collective_id=0, has_side_effects=True, vmem_limit_bytes=63 * 2**20),
        name="train",
    )(x, dy, w_gate, w_up, w_down)


def adamw(w, m, v, g):
    m = 0.9 * m + 0.1 * g
    v = 0.95 * v + 0.05 * g * g
    step = m * lax.rsqrt(v + 1e-8) + 0.1 * w
    return (w - 0.02 * step).astype(BF16), m, v


def solution(mesh):
    n = mesh.shape["dp"]

    def step(x, dy, *arrays):
        weights, m, v = (arrays[i : i + 3] for i in (0, 3, 6))
        ggu, gd, squares = train(mesh, x[0], dy[0], *weights)[:3]
        gradients = [g.astype(F32) for g in (ggu[:, 0], ggu[:, 1], gd)]
        count = n * sum(g.size for g in gradients)
        factor = jnp.minimum(1.0, 0.5 * lax.rsqrt(squares[0, 0] / count + 1e-30))
        new = [adamw(w.astype(F32), m, v, g * factor) for w, m, v, g in zip(weights, m, v, gradients, strict=True)]
        return tuple(one[which] for which in range(3) for one in new)

    states, cut = P(("rep", "dp"), None, None), P(None, "dp", None)
    return jax.shard_map(
        step,
        mesh=mesh,
        in_specs=(states, states) + (cut,) * 9,
        out_specs=(P("rep", "dp", None),) * 9,
        check_vma=False,
    )
```

time: 302 us -> 286 us (0.947)
  Pallas kernels: 290 us -> 275 us
    pallas_call x1, Pallas kernels: 290 us -> 275 us  [train(): pl.pallas_call(functools.partial(train_kernel, nz, math.isqrt(mesh.shape[...]
where the time goes in v3:
time: 286 us
  Pallas kernels  275 us (96%)
  other arithmetic  8.06 us (3%)
    pallas_call x1, Pallas kernels, train(): pl.pallas_call(functools.partial(train_kernel, nz, math.isqrt(mesh.shape[...  275 us
    convert_element_type x2, other arithmetic, adamw(): return ((w - 0.02 * step).astype(BF16), m, v)  8.06 us

profile of v3, /device:TPU:21, one launch (start us, length us, event | category | flops | bytes accessed | tf_op | source)
XLA Modules:
  0.0 285.7 jit_solution(9633106145936034636)
XLA Ops:
  0.6 0.0 copy-start
  0.7 274.8 %train.1 = (bf16[2,2,40,3456]{3,2,1,0:T(8,128)(2,1)}, bf16[2,216,640]{2,1,0:T(8,128)(2,1)}, f32[8,128]{1,0:T(8,128)}, bf16[2,9,2,640,384]{4,3,2,1,0:T(8,128)(2,1...) custom-call(bf16[1024,640]{1,0:T(8,128)(2,1)} %bitcast.25, ...), custom_call_target="tpu_custom_call" | custom-call | tf_op jit(solution)/shard_map/train/pallas_call | solution.py:607
  275.4 1.2 slice.10
  277.3 0.0 copy-done
  277.3 0.0 copy-start.1
  277.3 0.0 copy-start.2
  277.3 0.0 copy-start.3
  277.3 0.0 copy-start.4
  277.4 0.0 copy-start.5
  277.4 0.0 copy-start.6
  277.4 3.8 %fusion.8 = (bf16[2,216,640]{2,1,0:T(8,128)(2,1)}, f32[2,216,640]{2,1,0:T(8,128)}, f32[2,216,640]{2,1,0:T(8,128)}) fusion(bf16[2,216,640]{2,1,0:T(8,128)(2,1)S(1)} %copy-done, f32[]{:T(128)} %bitcast.2, bf16[2,216,640]{2,1,0:T(8,128)(2,1)} %get-tuple-element.14, f32[2,216,640]{2,1,0:T(8,128)} %param.21, f32[2,216,640]{2,1,0:T(8,128)} %param.18), kind=kLoop, calls=%fused_computation.17 | loop fusion | flops 4700160 | bytes 6082564 | tf_op jit(solution)/shard_map/convert_element_type | solution.py:637
  281.1 0.0 copy-done.1
  281.1 0.0 copy-done.2
  281.1 0.0 copy-done.3
  281.1 0.0 copy-done.4
  281.2 0.0 copy-done.5
  281.2 0.2 copy-done.6
  281.4 4.3 %fusion.2 = (bf16[2,40,3456]{2,1,0:T(8,128)(2,1)}, f32[2,40,3456]{2,1,0:T(8,128)}, f32[2,40,3456]{2,1,0:T(8,128)}, bf16[2,40,3456]{2,1,0:T(8,128)(2,1)}, f32[2,40,3456]{2,1,0:T(8,128)}, /*index=5*/f32[2,40,3456]{2,1,0:T(8,128)}) fusion(bf16[2,40,3456]{2,1,0:T(8,128)(2,1)S(1)} %copy-done.1, f32[]{:T(128)} %bitcast.2, f32[2,40,3456]{2,1,0:T(8,128)S(1)} %copy-done.3, ...), kind=kLoop, calls=%fused_computation.11 | loop fusion | flops 9400320 | bytes 12165124 | tf_op jit(solution)/shard_map/convert_element_type | solution.py:637
Async XLA Ops:
  0.6 276.7 %copy-start = (bf16[2,216,640]{2,1,0:T(8,128)(2,1)S(1)}, bf16[2,216,640]{2,1,0:T(8,128)(2,1)}, u32[]{:S(2)}) copy-start(bf16[2,216,640]{2,1,0:T(8,128)(2,1)} %wd.1) | copy-start | bytes 1658884
  277.3 3.8 %copy-start.1 = (bf16[2,40,3456]{2,1,0:T(8,128)(2,1)S(1)}, bf16[2,40,3456]{2,1,0:T(8,128)(2,1)}, u32[]{:S(2)}) copy-start(bf16[2,40,3456]{2,1,0:T(8,128)(2,1)} %wg.1) | copy-start | bytes 1658884
  277.3 3.8 %copy-start.2 = (bf16[2,40,3456]{2,1,0:T(8,128)(2,1)S(1)}, bf16[2,40,3456]{2,1,0:T(8,128)(2,1)}, u32[]{:S(2)}) copy-start(bf16[2,40,3456]{2,1,0:T(8,128)(2,1)} %wu.1) | copy-start | bytes 1658884
  277.3 3.8 %copy-start.3 = (f32[2,40,3456]{2,1,0:T(8,128)S(1)}, f32[2,40,3456]{2,1,0:T(8,128)}, u32[]{:S(2)}) copy-start(f32[2,40,3456]{2,1,0:T(8,128)} %param.19) | copy-start | bytes 3317764
  277.3 3.8 %copy-start.4 = (f32[2,40,3456]{2,1,0:T(8,128)S(1)}, f32[2,40,3456]{2,1,0:T(8,128)}, u32[]{:S(2)}) copy-start(f32[2,40,3456]{2,1,0:T(8,128)} %param.16) | copy-start | bytes 3317764
  277.4 3.8 %copy-start.5 = (f32[2,40,3456]{2,1,0:T(8,128)S(1)}, f32[2,40,3456]{2,1,0:T(8,128)}, u32[]{:S(2)}) copy-start(f32[2,40,3456]{2,1,0:T(8,128)} %param.20) | copy-start | bytes 3317764
  277.4 4.0 %copy-start.6 = (f32[2,40,3456]{2,1,0:T(8,128)S(1)}, f32[2,40,3456]{2,1,0:T(8,128)}, u32[]{:S(2)}) copy-start(f32[2,40,3456]{2,1,0:T(8,128)} %param.17) | copy-start | bytes 3317764

commit v4 on v3

--- a/solution.py
+++ b/solution.py
@@ -11,7 +11,9 @@
 MESH = pl.DeviceIdType.MESH
 ANY = pl.BlockSpec(memory_space=pltpu.HBM)
 F32, BF16 = jnp.float32, jnp.bfloat16
+LAG = 3
 SK = 2
+DSLOTS = 8
 SLOTS = 8
 GSLOTS = 16
 RSLOTS = 8
@@ -20,8 +22,8 @@
 GSK = 2
 DCH = 3
 CHUNKS = 9
-SPREAD = 1
 THREE = 3
+PARTS = 2
 PIECES = 9
 
 
@@ -37,9 +39,9 @@
     return lax.dot_general(a, b, (((0,), (0,)), ((), ())), preferred_element_type=F32)
 
 
-def train_kernel(nz, ny, x, dy, wg, wu, wd, ggu, gd, sqo, WGU, WD, GUH, DGH, AH, ATH,
+def train_kernel(nz, ny, x, dy, wg, wu, wd, ggu, gd, sqo, WGU, WD, GUH, DGH, ACTH, AH, ATH,
                  H, DY, A, AT, DACC, WC, WDC, GUS, DGU, ACT, TS, R, TD, RD, BG, BD, FG, FD, SQ, SQALL, sgu, sd,
-                 load_sem, w_sem, gu_sem, dg_sem, own_sem, g_recv, g_sib, g_send, g_par,
+                 load_sem, w_sem, gu_sem, dg_sem, act_sem, own_sem, g_recv, g_sib, g_send, g_par,
                  r_send, r_recv, rd_send, rd_recv, ring_send, ring_recv, dring_send, dring_recv, fin_send, dfin_send, fin_recv, sq_send, sq_recv):
     me = lax.axis_index("dp")
     z, c = me // 2, me % 2
@@ -59,14 +61,23 @@
     dhalf = (drow // 16 + 1) * 8
     gpar = GSK * half + GPAR
     gdone = gpar + GDONE
-    UF = DCH + gdone + 1
-    U1 = UF + CHUNKS
+    UF = gdone + 1
+    UE = UF + CHUNKS + DCH - 1
+    U1 = UE + CHUNKS // THREE
     UB = U1 + CHUNKS
-    UC = UB + CHUNKS // THREE + 1
-    G1, G0, D1, D0 = 1, UC - U1 + 1, CHUNKS + 1, UC - U1 + CHUNKS + 1
+    UD = UB + CHUNKS // THREE
+    UC = UD + 2
+    G1, G0, D1 = 1, UC - U1 + 1, UC - U1 + 1 - items
+
+    early = gper + DCH
+    gsteps = early + 2 * (gtotal - 1 - early) + gdone + 1
 
     def gathered(u):
-        return jnp.where(u < UF, u, UF + lax.div(4 * (u - UF), 3))
+        return jnp.where(u < UE, u, UE + jnp.where(u < U1, lax.div(4 * (u - UE), 3), 4 * (U1 - UE) // 3 + 2 * (u - U1)))
+
+    def started(t):
+        late = t - early
+        return (t >= 0) & ((late <= 0) | ((lax.rem(late, 2) == 0) & (t < gsteps - gdone))), jnp.where(late > 0, early + lax.div(late, 2), t)
 
     rep = lax.axis_index("rep")
     gx, gy = rep // ny, rep % ny
@@ -116,9 +127,11 @@
         lax.fori_loop(0, tokens // 128, rows, 0)
 
     def chunk(q):
-        layer = jnp.where(q >= gper, 1, 0)
-        r = q - layer * gper
-        return layer, r < DCH, jnp.where(r < DCH, r, r - DCH)
+        second = q >= gper
+        r = jnp.where(second, q - gper, q)
+        down = jnp.where(second, r, r - CHUNKS)
+        is_down = (down >= 0) & (down < DCH)
+        return jnp.where(second, 1, 0), is_down, jnp.where(is_down, down, jnp.where(second, r - DCH, r))
 
     def piece(q, blk, part, own, fn):
         layer, is_down, r = chunk(q)
@@ -157,21 +170,22 @@
         remote(src, dst, g_send.at[lax.rem(q, GSLOTS)], g_par.at[lax.rem(q, GSLOTS)], {"rep": to, "dp": me}).start()
 
     def gather_step(t):
-        @pl.when(t < gtotal)
-        def _():
+        def start(q):
             def own(src, dst):
-                to_next(t, 0, 1, src, dst)
-                to_next(t, 1, 1, src, dst)
-            piece(t, me, 0, True, own)
+                to_next(q, 0, 1, src, dst)
+                to_next(q, 1, 1, src, dst)
+            piece(q, me, 0, True, own)
             def whole(src, dst):
-                to_sibling(t, src, dst)
-                pltpu.make_async_copy(src, dst, own_sem.at[lax.rem(t, GSLOTS)]).start()
-            piece(t, me, 2, True, whole)
+                to_sibling(q, src, dst)
+                pltpu.make_async_copy(src, dst, own_sem.at[lax.rem(q, GSLOTS)]).start()
+            piece(q, me, 2, True, whole)
+        there, first = started(t)
+        pl.when(there)(lambda: start(first))
         for h in range(1, half + 1):
-            q = t - GSK * h
+            there, q = started(t - GSK * h)
             for way in (0, 1):
                 longer = lax.rem(q, 2) == way
-                ok = (q >= 0) & (q < gtotal)
+                ok = there
                 if h == half:
                     ok = ok & longer
                 @pl.when(ok)
@@ -186,8 +200,8 @@
                                 to_next(q, way, h + 1, src, dst)
                         to_beside(q, src, dst)
                     piece(q, block(z - h if way == 0 else z + h), 0, False, go)
-        q = t - gpar
-        @pl.when((q >= 0) & (q < gtotal))
+        there, q = started(t - gpar)
+        @pl.when(there)
         def _():
             layer, is_down, r = chunk(q)
             slot = lax.rem(q, GSLOTS)
@@ -202,8 +216,8 @@
                 wait(WGU.at[layer, 0, 0, pl.ds(0, (nz - 1) * rgu), :], g_par.at[slot])
             for h in range(1, nz):
                 piece(q, block(z + h), 2, False, lambda src, dst: to_sibling(q, src, dst))
-        q = t - gdone
-        @pl.when((q >= 0) & (q < gtotal))
+        there, q = started(t - gdone)
+        @pl.when(there)
         def _():
             layer, is_down, r = chunk(q)
             slot = lax.rem(q, GSLOTS)
@@ -224,10 +238,10 @@
                     waited(WGU.at[layer, 0, :, pl.ds(0, k * rgu), :], sem)
 
     def work(u):
-        ks = [u - first for first in (UF, U1, UB, UC)]
-        on = functools.reduce(jnp.logical_or, [(k >= 0) & (k < (CHUNKS // THREE if first == UB else CHUNKS)) for k, first in zip(ks, (UF, U1, UB, UC))])
-        pick = lambda a, b, c, d: jnp.where(u < U1, a, jnp.where(u < UB, b, jnp.where(u < UC, c, d)))
-        return on, pick(0, 1, 2, 3), pick(*ks)
+        ks = [u - first for first in (UF, U1, UC)]
+        on = functools.reduce(jnp.logical_or, [(k >= 0) & (k < CHUNKS) for k in ks])
+        pick = lambda a, b, c: jnp.where(u < UE, a, jnp.where(u < UC, b, c))
+        return on, pick(0, 1, 3), pick(*ks)
 
     def loads(u):
         on, kind, j = work(u)
@@ -236,7 +250,7 @@
         return (
             (on & (kind < 2), pltpu.make_async_copy(WGU.at[layer, j, 0], WC.at[slot, :, pl.ds(0, cw)], w_sem.at[slot, 0])),
             (on & (kind < 2), pltpu.make_async_copy(WGU.at[layer, j, 1], WC.at[slot, :, pl.ds(cw, cw)], w_sem.at[slot, 1])),
-            (on & (kind != 2), pltpu.make_async_copy(WD.at[layer, pl.ds(pl.multiple_of(j * cw, 128), cw), :], WDC.at[slot], w_sem.at[slot, 2])),
+            (on & (kind > 0), pltpu.make_async_copy(WD.at[layer, pl.ds(pl.multiple_of(j * cw, 128), cw), :], WDC.at[slot], w_sem.at[slot, 2])),
             (on & (kind == 3), pltpu.make_async_copy(GUH.at[j], GUS.at[slot], w_sem.at[slot, 4])),
         )
 
@@ -247,27 +261,69 @@
         @pl.when(j >= 2)
         def _():
             kept(j, slot, GUS, GUH, gu_sem).wait()
+            kept(j, slot, ACT, ACTH, act_sem).wait()
         gu = mm(A[...], WC[slot])
         GUS[slot] = gu
         kept(j, slot, GUS, GUH, gu_sem).start()
         g, up = gu[:, :cw], gu[:, cw:]
-        ACT[...] = (g * jax.nn.sigmoid(g) * up).astype(BF16)
-        @pl.when(j == 0)
-        def _():
-            DACC[...] = jnp.zeros_like(DACC)
-        DACC[...] += mm(ACT[...], WDC[slot])
-
-    def down_gradient(layer, j):
-        TD[layer, pl.ds(pl.multiple_of(j * cw, 128), cw), :] = mm_tn(ACT[...], DY[...]).astype(BF16)
-
-    def backward(gu, j, slot):
-        g, up = gu[:, :cw], gu[:, cw:]
-        back = mm_nt(DY[...], WDC[slot]).astype(BF16).astype(F32)
-        sg = jax.nn.sigmoid(g)
-        s = g * sg
-        ACT[...] = (s * up).astype(BF16)
-        DGU[slot, :, :cw] = (back * up * (sg + s * (1.0 - sg))).astype(BF16)
-        DGU[slot, :, cw:] = (back * s).astype(BF16)
+        ACT[slot] = (g * jax.nn.sigmoid(g) * up).astype(BF16)
+        kept(j, slot, ACT, ACTH, act_sem).start()
+
+    def nth(m):
+        return jnp.where(m < 2, CHUNKS - 2 + m, CHUNKS - 1 - m)
+
+    def down_rows(m, slot):
+        return pltpu.make_async_copy(WD.at[0, pl.ds(pl.multiple_of(nth(m) * cw, 128), cw), :], WDC.at[slot], w_sem.at[slot, 2])
+
+    def forward_down(step):
+        def one(i, _):
+            m = THREE * step + i
+            slot = lax.rem(m + UF + CHUNKS, 2)
+            act = lambda k: pltpu.make_async_copy(ACTH.at[k], ACT.at[slot], act_sem.at[slot])
+            down_rows(m, slot).wait()
+            @pl.when(m >= 2)
+            def _():
+                act(0).wait()
+            @pl.when(m == 0)
+            def _():
+                DACC[...] = jnp.zeros_like(DACC)
+            DACC[...] += mm(ACT[slot], WDC[slot])
+            @pl.when(m + 2 < CHUNKS)
+            def _():
+                down_rows(m + 2, slot).start()
+                act(nth(m + 2)).start()
+            return 0
+        lax.fori_loop(0, THREE, one, 0)
+
+    def down_gradient(layer, j, slot):
+        TD[layer, pl.ds(pl.multiple_of(j * cw, 128), cw), :] = mm_tn(ACT[slot], DY[...]).astype(BF16)
+
+    def kept_act(k):
+        slot = lax.rem(k, 2)
+        return pltpu.make_async_copy(ACTH.at[k], ACT.at[slot], act_sem.at[slot])
+
+    def down_gradients(first, last):
+        def one(k, _):
+            kept_act(k).wait()
+            down_gradient(0, k, lax.rem(k, 2))
+            @pl.when(k + 2 < CHUNKS)
+            def _():
+                kept_act(k + 2).start()
+            return 0
+        lax.fori_loop(first, last, one, 0)
+
+    def backward(products, j, slot, with_act):
+        for first in range(0, tokens, tokens // PARTS):
+            rs = pl.ds(first, tokens // PARTS)
+            gu = products(rs)
+            g, up = gu[:, :cw], gu[:, cw:]
+            back = mm_nt(DY[rs, :], WDC[slot]).astype(BF16).astype(F32)
+            sg = jax.nn.sigmoid(g)
+            s = g * sg
+            if with_act:
+                ACT[slot, rs, :] = (s * up).astype(BF16)
+            DGU[slot, rs, :cw] = (back * up * (sg + s * (1.0 - sg))).astype(BF16)
+            DGU[slot, rs, cw:] = (back * s).astype(BF16)
         t = mm(AT[...], DGU[slot]).astype(BF16)
         TS[0, j] = t[:, :cw]
         TS[1, j] = t[:, cw:]
@@ -276,13 +332,13 @@
         @pl.when(j >= 2)
         def _():
             kept(j, slot, DGU, DGH, dg_sem).wait()
-        backward(mm(A[...], WC[slot]), j, slot)
+        backward(lambda rs: mm(A[rs, :], WC[slot]), j, slot, True)
         @pl.when(j < CHUNKS - 2)
         def _():
             kept(j, slot, DGU, DGH, dg_sem).start()
 
     def first_layer(j, slot):
-        backward(GUS[slot], j, slot)
+        backward(lambda rs: GUS[slot, rs, :], j, slot, False)
 
     def input_gradient(step):
         def again(k, slot):
@@ -341,19 +397,16 @@
         e.buf, e.sent, e.come = BG, ring_send, ring_recv
         return e
 
-    def d_item(t, s, layer):
+    def d_item(t, s):
         e = Item()
-        if layer == 1:
-            i = t - D1 - SK * s
-            e.valid = (i >= 0) & (i < SPREAD * items) & (lax.rem(i, SPREAD) == 0)
-            k = lax.div(i, SPREAD)
-        else:
-            k = t - D0 - s
-            e.valid = (k >= 0) & (k < items)
-        e.p = 2 * k + (1 - c if layer == 1 else c)
-        e.valid = e.valid & (e.p < PIECES)
-        e.k, e.layer, e.odd, e.gu = k, layer, lax.rem(k, 2), False
-        e.slot = k
+        i = t - D1 - SK * s
+        e.valid = (i >= 0) & (i < 2 * items)
+        e.layer = jnp.where(i < items, 1, 0)
+        k = i - (1 - e.layer) * items
+        mine = jnp.where(e.layer == c, 0, 1)
+        e.p, e.theirs = 2 * k + mine, 2 * k + 1 - mine
+        e.sends, e.valid = e.valid & (e.theirs < PIECES), e.valid & (e.p < PIECES)
+        e.i, e.slot, e.odd, e.gu = i, lax.rem(i, DSLOTS), lax.rem(k, 2), False
         e.buf, e.sent, e.come = BD, dring_send, dring_recv
         return e
 
@@ -362,7 +415,7 @@
             rs = pl.ds(pl.multiple_of(zz * (2 * rgu), 16), 2 * rgu)
             return TS[c, e.r, rs, :].astype(F32) + R[e.r, rs, :].astype(F32)
         rs = pl.ds(pl.multiple_of(zz * crd + e.p * prow, 16), prow)
-        return TD[e.layer, rs, :].astype(F32) + RD[e.slot, zz].astype(F32)
+        return TD[e.layer, rs, :].astype(F32) + RD[e.i, zz].astype(F32)
 
     def around(zz):
         return jnp.where(zz >= nz, zz - nz, jnp.where(zz < 0, zz + nz, zz))
@@ -447,71 +500,56 @@
                 else:
                     wait(FD.at[e.slot, b], dfin_send.at[b, e.slot])
 
-    streams = (gu_item, lambda t, s: d_item(t, s, 1), lambda t, s: d_item(t, s, 0))
+    streams = (gu_item, d_item)
 
     def send_terms(t):
         e = gu_item(t + 1, 0)
         @pl.when(e.valid)
         def _():
             remote(TS.at[1 - c, e.r], R.at[e.r], r_send, r_recv.at[e.r], sibling).start()
-        for layer in (1, 0):
-            e = d_item(t + 1, 0, layer)
-            p = 2 * e.k + (c if layer == 1 else 1 - c)
-            there = d_valid(t + 1, layer) & (p < PIECES)
-            @pl.when(there)
-            def _():
-                for zz in range(nz):
-                    rs = pl.ds(pl.multiple_of(zz * crd + p * prow, 16), prow)
-                    remote(TD.at[layer, rs, :], RD.at[e.slot, zz], rd_send, rd_recv.at[e.slot], sibling).start()
-
-    def d_valid(t, layer):
-        if layer == 1:
-            i = t - D1
-            return (i >= 0) & (i < SPREAD * items) & (lax.rem(i, SPREAD) == 0)
-        return (t >= D0) & (t < D0 + items)
+        f = d_item(t + 1, 0)
+        @pl.when(f.sends)
+        def _():
+            for zz in range(nz):
+                rs = pl.ds(pl.multiple_of(zz * crd + f.theirs * prow, 16), prow)
+                remote(TD.at[f.layer, rs, :], RD.at[f.i, zz], rd_send, rd_recv.at[f.i], sibling).start()
 
     def terms_sent(t):
         e = gu_item(t + 1, 0)
         @pl.when(e.valid)
         def _():
             wait(R.at[e.r], r_send)
-        for layer in (1, 0):
-            e = d_item(t + 1, 0, layer)
-            p = 2 * e.k + (c if layer == 1 else 1 - c)
-            @pl.when(d_valid(t + 1, layer) & (p < PIECES))
-            def _():
-                wait(RD.at[e.slot], rd_send)
+        f = d_item(t + 1, 0)
+        @pl.when(f.sends)
+        def _():
+            wait(RD.at[f.i], rd_send)
 
     def reduce_step(t):
         terms_sent(t - 1)
         for which in streams:
             for s in range(half):
-                stage_sent(which(t - 1, s), s)
+                stage_sent(which(t - LAG, s), s)
             last_sent(which(t - 1, half))
-        for some in (streams[:2], streams[2:]):
-            for which in some:
-                last(which(t, half))
-            for s in reversed(range(half)):
-                for which in some:
-                    e = which(t, s)
-                    if s == 0:
-                        @pl.when(e.valid)
-                        def _():
-                            if e.gu:
-                                wait(R.at[e.r], r_recv.at[e.r])
-                            else:
-                                wait(RD.at[e.slot], rd_recv.at[e.slot])
-                    stage(e, s)
-
-    normalize(H, True)
+        for which in streams:
+            last(which(t, half))
+        for s in reversed(range(half)):
+            for which in streams:
+                e = which(t, s)
+                if s == 0:
+                    @pl.when(e.valid)
+                    def _():
+                        if e.gu:
+                            wait(R.at[e.r], r_recv.at[e.r])
+                        else:
+                            wait(RD.at[e.i], rd_recv.at[e.i])
+                stage(e, s)
+
     keep = (pltpu.make_async_copy(A, AH, load_sem.at[0]), pltpu.make_async_copy(AT, ATH, load_sem.at[1]))
     back = (pltpu.make_async_copy(AH, A, load_sem.at[0]), pltpu.make_async_copy(ATH, AT, load_sem.at[1]))
-    for copy in keep:
-        copy.start()
 
     def step(u, _):
         t = u - U1
-        @pl.when(gathered(u) < gtotal + gdone)
+        @pl.when(gathered(u) < gsteps)
         def _():
             def one(tg, _):
                 gather_step(tg)
@@ -523,12 +561,25 @@
 
         on, kind, j = work(u)
         slot = lax.rem(u, 2)
-        @pl.when((u == UF + CHUNKS) | (u == UF + CHUNKS + 1))
-        def _():
-            kept(0, slot, GUS, GUH, gu_sem).wait()
-        for there, copy in loads(u + 1):
-            @pl.when(there)
-            def _():
+        @pl.when(u == UE - 1)
+        def _():
+            for m in range(2):
+                down_rows(m, lax.rem(m + UF + CHUNKS, 2)).start()
+        @pl.when(u == UE)
+        def _():
+            for m in range(2):
+                kept(0, m, GUS, GUH, gu_sem).wait()
+                kept(0, m, ACT, ACTH, act_sem).wait()
+        def fetch():
+            for there, copy in loads(u + 1):
+                @pl.when(there)
+                def _():
+                    copy.start()
+        pl.when(u != U1 - 1)(fetch)
+        @pl.when(u == 2)
+        def _():
+            normalize(H, True)
+            for copy in keep:
                 copy.start()
         @pl.when(u == U1)
         def _():
@@ -539,7 +590,9 @@
         def _():
             for copy in back:
                 copy.start()
-        @pl.when(u == UC - 1)
+            for k in range(2):
+                kept_act(k).start()
+        @pl.when(u == UD)
         def _():
             between()
             for copy in back:
@@ -562,16 +615,20 @@
             send_terms(t)
         @pl.when(on & (kind == 1))
         def _():
-            down_gradient(1, j)
-        @pl.when(on & (kind == 2))
-        def _():
-            input_gradient(j)
-        @pl.when(on & (kind == 3))
-        def _():
-            down_gradient(0, j)
+            down_gradient(1, j, slot)
+        @pl.when((u >= UE) & (u < U1))
+        def _():
+            forward_down(u - UE)
+        pl.when(u == U1 - 1)(fetch)
+        @pl.when((u >= UB) & (u < UD))
+        def _():
+            input_gradient(u - UB)
+        @pl.when((u >= UD) & (u < UC))
+        def _():
+            down_gradients(jnp.where(u == UD, 0, CHUNKS // 2), jnp.where(u == UD, CHUNKS // 2, CHUNKS))
         return 0
 
-    lax.fori_loop(0, U1 + D0 + items + half + 1, step, 0)
+    lax.fori_loop(0, U1 + G0 + CHUNKS + SK * half + 1, step, 0)
 
     for i in range(1, n):
         remote(SQ, SQALL.at[me], sq_send, sq_recv, {"dp": lax.rem(me + i, n)}).start()
@@ -588,7 +645,7 @@
     acc = SQ[...]
     for i in range(1, n):
         acc = acc + SQALL[lax.rem(me + i, n)]
-    sqo[...] = jnp.full((8, 128), jnp.sum(acc), F32)
+    sqo[0, 0] = jnp.sum(acc)
     wait(SQALL.at[pl.ds(0, n - 1)], sq_send)
 
 
@@ -607,23 +664,23 @@
     return pl.pallas_call(
         functools.partial(train_kernel, nz, math.isqrt(mesh.shape["rep"])),
         out_shape=(
-            shape((layers, 2, rgu, ff), BF16), shape((layers, rd, d), BF16), shape((8, 128), F32),
+            shape((layers, 2, rgu, ff), BF16), shape((layers, rd, d), BF16), shape((1, 1), F32),
             shape((layers, CHUNKS, 2, d, cw), BF16), shape((layers, ff, d), BF16),
-            shape((CHUNKS, tokens, 2 * cw), F32), shape((CHUNKS, tokens, 2 * cw), BF16),
+            shape((CHUNKS, tokens, 2 * cw), F32), shape((CHUNKS, tokens, 2 * cw), BF16), shape((CHUNKS, tokens, cw), BF16),
             shape((tokens, d), BF16), shape((d, tokens), BF16),
         ),
         in_specs=[ANY] * 5,
-        out_specs=(ANY, ANY, pl.BlockSpec(memory_space=pltpu.VMEM), ANY, ANY, ANY, ANY, ANY, ANY),
+        out_specs=(ANY, ANY, pl.BlockSpec(memory_space=pltpu.SMEM), ANY, ANY, ANY, ANY, ANY, ANY, ANY),
         scratch_shapes=[
             V((tokens, d), BF16), V((tokens, d), BF16), V((tokens, d), BF16), V((d, tokens), BF16), V((tokens, d), F32),
-            V((2, d, 2 * cw), BF16), V((2, cw, d), BF16), V((2, tokens, 2 * cw), F32), V((2, tokens, 2 * cw), BF16), V((tokens, cw), BF16),
-            V((2, CHUNKS, d, cw), BF16), V((CHUNKS, d, cw), BF16), V((layers, ff, d), BF16), V((items, nz, prow, d), BF16),
-            V((2, half + 1, SLOTS, 2 * rgu, cw), BF16), V((2, half + 1, items, prow, d), BF16),
-            V((SLOTS, 2, rgu, cw), BF16), V((items, 2, prow // 2, d), BF16),
+            V((2, d, 2 * cw), BF16), V((2, cw, d), BF16), V((2, tokens, 2 * cw), F32), V((2, tokens, 2 * cw), BF16), V((2, tokens, cw), BF16),
+            V((2, CHUNKS, d, cw), BF16), V((CHUNKS, d, cw), BF16), V((layers, ff, d), BF16), V((2 * items, nz, prow, d), BF16),
+            V((2, half + 1, SLOTS, 2 * rgu, cw), BF16), V((2, half + 1, DSLOTS, prow, d), BF16),
+            V((SLOTS, 2, rgu, cw), BF16), V((DSLOTS, 2, prow // 2, d), BF16),
             V((8, 128), F32), V((n, 8, 128), F32), V((layers, CHUNKS, 2, rgu, cw), BF16), V((layers, rd, d), BF16),
-            S((4,)), S((2, 5)), S((2,)), S((2,)), S((GSLOTS,)), S((2, half, RSLOTS)), S((GSLOTS,)), S((GSLOTS,)), S((GSLOTS,)),
-            S, S((CHUNKS,)), S, S((items,)), S((2, half, SLOTS)), S((2, half, SLOTS)), S((2, half, items)), S((2, half, items)),
-            S((2, SLOTS)), S((2, items)), S((layers, 2)), S, S,
+            S((4,)), S((2, 5)), S((2,)), S((2,)), S((2,)), S((GSLOTS,)), S((2, half, RSLOTS)), S((GSLOTS,)), S((GSLOTS,)), S((GSLOTS,)),
+            S, S((CHUNKS,)), S, S((2 * items,)), S((2, half, SLOTS)), S((2, half, SLOTS)), S((2, half, DSLOTS)), S((2, half, DSLOTS)),
+            S((2, SLOTS)), S((2, DSLOTS)), S((layers, 2)), S, S,
         ],
         compiler_params=pltpu.CompilerParams(collective_id=0, has_side_effects=True, vmem_limit_bytes=63 * 2**20),
         name="train",

time: 286 us -> 265 us (0.927)
  Pallas kernels: 275 us -> 255 us
    pallas_call x1, Pallas kernels: 275 us -> 255 us  [train(): pl.pallas_call(functools.partial(train_kernel, nz, math.isqrt(mesh.shape[...]
where the time goes in v4:
time: 265 us; the launch traced here: 264 us
  Pallas kernels  255 us (96%)
  other arithmetic  8.06 us (3%)
    pallas_call x1, Pallas kernels, train(): pl.pallas_call(functools.partial(train_kernel, nz, math.isqrt(mesh.shape[...  255 us
    convert_element_type x2, other arithmetic, adamw(): return ((w - 0.02 * step).astype(BF16), m, v)  8.06 us

profile of v4, /device:TPU:21, one launch (start us, length us, event | category | flops | bytes accessed | tf_op | source)
XLA Modules:
  0.0 264.4 jit_solution(134579969994154773)
XLA Ops:
  0.6 0.0 copy-start
  0.7 254.6 %train.1 = (bf16[2,2,40,3456]{3,2,1,0:T(8,128)(2,1)}, bf16[2,216,640]{2,1,0:T(8,128)(2,1)}, f32[1,1]{1,0:T(1,128)}, bf16[2,9,2,640,384]{4,3,2,1,0:T(8,128)(2,1)}...) custom-call(bf16[1024,640]{1,0:T(8,128)(2,1)} %bitcast.25, ...), custom_call_target="tpu_custom_call" | custom-call | tf_op jit(solution)/shard_map/train/pallas_call | solution.py:664
  256.0 0.0 copy-done
  256.0 0.0 copy-start.1
  256.0 0.0 copy-start.2
  256.0 0.0 copy-start.3
  256.0 0.0 copy-start.4
  256.0 0.0 copy-start.5
  256.0 0.0 copy-start.6
  256.1 3.8 %fusion.8 = (bf16[2,216,640]{2,1,0:T(8,128)(2,1)}, f32[2,216,640]{2,1,0:T(8,128)}, f32[2,216,640]{2,1,0:T(8,128)}) fusion(bf16[2,216,640]{2,1,0:T(8,128)(2,1)S(1)} %copy-done, f32[]{:T(128)} %bitcast.2, bf16[2,216,640]{2,1,0:T(8,128)(2,1)} %get-tuple-element.14, f32[2,216,640]{2,1,0:T(8,128)} %param.21, f32[2,216,640]{2,1,0:T(8,128)} %param.18), kind=kLoop, calls=%fused_computation.17 | loop fusion | flops 4700160 | bytes 6082564 | tf_op jit(solution)/shard_map/convert_element_type | solution.py:694
  259.8 0.0 copy-done.1
  259.8 0.0 copy-done.2
  259.8 0.0 copy-done.3
  259.8 0.0 copy-done.4
  259.8 0.0 copy-done.5
  259.8 0.2 copy-done.6
  260.0 4.3 %fusion.2 = (bf16[2,40,3456]{2,1,0:T(8,128)(2,1)}, f32[2,40,3456]{2,1,0:T(8,128)}, f32[2,40,3456]{2,1,0:T(8,128)}, bf16[2,40,3456]{2,1,0:T(8,128)(2,1)}, f32[2,40,3456]{2,1,0:T(8,128)}, /*index=5*/f32[2,40,3456]{2,1,0:T(8,128)}) fusion(bf16[2,40,3456]{2,1,0:T(8,128)(2,1)S(1)} %copy-done.1, f32[]{:T(128)} %bitcast.2, f32[2,40,3456]{2,1,0:T(8,128)S(1)} %copy-done.3, ...), kind=kLoop, calls=%fused_computation.11 | loop fusion | flops 9400320 | bytes 12165124 | tf_op jit(solution)/shard_map/convert_element_type | solution.py:694
Async XLA Ops:
  0.6 255.3 %copy-start = (bf16[2,216,640]{2,1,0:T(8,128)(2,1)S(1)}, bf16[2,216,640]{2,1,0:T(8,128)(2,1)}, u32[]{:S(2)}) copy-start(bf16[2,216,640]{2,1,0:T(8,128)(2,1)} %wd.1) | copy-start | bytes 1658884
  256.0 3.8 %copy-start.1 = (bf16[2,40,3456]{2,1,0:T(8,128)(2,1)S(1)}, bf16[2,40,3456]{2,1,0:T(8,128)(2,1)}, u32[]{:S(2)}) copy-start(bf16[2,40,3456]{2,1,0:T(8,128)(2,1)} %wg.1) | copy-start | bytes 1658884
  256.0 3.8 %copy-start.2 = (bf16[2,40,3456]{2,1,0:T(8,128)(2,1)S(1)}, bf16[2,40,3456]{2,1,0:T(8,128)(2,1)}, u32[]{:S(2)}) copy-start(bf16[2,40,3456]{2,1,0:T(8,128)(2,1)} %wu.1) | copy-start | bytes 1658884
  256.0 3.8 %copy-start.3 = (f32[2,40,3456]{2,1,0:T(8,128)S(1)}, f32[2,40,3456]{2,1,0:T(8,128)}, u32[]{:S(2)}) copy-start(f32[2,40,3456]{2,1,0:T(8,128)} %param.19) | copy-start | bytes 3317764
  256.0 3.8 %copy-start.4 = (f32[2,40,3456]{2,1,0:T(8,128)S(1)}, f32[2,40,3456]{2,1,0:T(8,128)}, u32[]{:S(2)}) copy-start(f32[2,40,3456]{2,1,0:T(8,128)} %param.16) | copy-start | bytes 3317764
  256.0 3.8 %copy-start.5 = (f32[2,40,3456]{2,1,0:T(8,128)S(1)}, f32[2,40,3456]{2,1,0:T(8,128)}, u32[]{:S(2)}) copy-start(f32[2,40,3456]{2,1,0:T(8,128)} %param.20) | copy-start | bytes 3317764
  256.0 4.0 %copy-start.6 = (f32[2,40,3456]{2,1,0:T(8,128)S(1)}, f32[2,40,3456]{2,1,0:T(8,128)}, u32[]{:S(2)}) copy-start(f32[2,40,3456]{2,1,0:T(8,128)} %param.17) | copy-start | bytes 3317764

commit v5 on v4

--- a/solution.py
+++ b/solution.py
@@ -104,11 +104,11 @@
             pltpu.make_async_copy(w.at[:, :, j * cw : (j + 1) * cw], sgu.at[:, j, m], load_sem.at[3]).start()
 
     barrier = pltpu.get_barrier_semaphore()
-    for i in range(1, n):
-        pl.semaphore_signal(barrier, inc=1, device_id={"dp": lax.rem(me + i, n)}, device_id_type=MESH)
+    for to in (up, down, sibling):
+        pl.semaphore_signal(barrier, inc=1, device_id=to, device_id_type=MESH)
     for to in (beside_x, beside_y):
         pl.semaphore_signal(barrier, inc=1, device_id={"rep": to, "dp": me}, device_id_type=MESH)
-    pl.semaphore_wait(barrier, n + 1)
+    pl.semaphore_wait(barrier, 5)
     for cp in first:
         cp.wait()
     pltpu.make_async_copy(WGU.at[:, :, :, :rgu, :], sgu, load_sem.at[3]).wait()
@@ -163,11 +163,21 @@
         remote(src, dst, g_send.at[lax.rem(q, GSLOTS)], g_sib.at[lax.rem(q, GSLOTS)], sibling).start()
 
     def to_next(q, way, hop, src, dst):
-        remote(src, dst, g_send.at[lax.rem(q, GSLOTS)], g_recv.at[way, hop - 1, lax.rem(q, RSLOTS)], (up, down)[way]).start()
+        remote(src, dst, g_send.at[lax.rem(q, GSLOTS)], g_recv.at[hop - 1, lax.rem(q, RSLOTS)], (up, down)[way]).start()
 
     def to_beside(q, src, dst):
         to = jnp.where(lax.rem(q, 2) == 0, beside_y, beside_x)
         remote(src, dst, g_send.at[lax.rem(q, GSLOTS)], g_par.at[lax.rem(q, GSLOTS)], {"rep": to, "dp": me}).start()
+
+    def come(q, part, count, sem):
+        layer, is_down, _ = chunk(q)
+        for first, rows in ((0, dhalf), (1, drow - dhalf)):
+            @pl.when(is_down & (lax.rem(diagonal + part, 2) == first))
+            def _():
+                wait(WD.at[layer, pl.ds(0, count * rows), :], sem)
+        @pl.when(jnp.logical_not(is_down))
+        def _():
+            wait(WGU.at[layer, 0, 0, pl.ds(0, count * rgu), :], sem)
 
     def gather_step(t):
         def start(q):
@@ -183,37 +193,28 @@
         pl.when(there)(lambda: start(first))
         for h in range(1, half + 1):
             there, q = started(t - GSK * h)
-            for way in (0, 1):
-                longer = lax.rem(q, 2) == way
-                ok = there
-                if h == half:
-                    ok = ok & longer
-                @pl.when(ok)
-                def _():
+            @pl.when(there)
+            def _():
+                come(q, 0, 2 if h < half else 1, g_recv.at[h - 1, lax.rem(q, RSLOTS)])
+                for way in (0, 1):
                     def go(src, dst):
-                        remote(src, dst, g_send.at[0], g_recv.at[way, h - 1, lax.rem(q, RSLOTS)], sibling).wait_recv()
                         if h < half - 1:
                             to_next(q, way, h + 1, src, dst)
                         elif h == half - 1:
-                            @pl.when(longer)
+                            @pl.when(lax.rem(q, 2) == way)
                             def _():
                                 to_next(q, way, h + 1, src, dst)
                         to_beside(q, src, dst)
-                    piece(q, block(z - h if way == 0 else z + h), 0, False, go)
+                    def take():
+                        piece(q, block(z - h if way == 0 else z + h), 0, False, go)
+                    if h < half:
+                        take()
+                    else:
+                        pl.when(lax.rem(q, 2) == way)(take)
         there, q = started(t - gpar)
         @pl.when(there)
         def _():
-            layer, is_down, r = chunk(q)
-            slot = lax.rem(q, GSLOTS)
-            @pl.when(is_down)
-            def _():
-                for theirs in range(2):
-                    @pl.when(diagonal != theirs)
-                    def _():
-                        wait(WD.at[layer, pl.ds(0, (nz - 1) * (drow - dhalf if theirs else dhalf)), :], g_par.at[slot])
-            @pl.when(jnp.logical_not(is_down))
-            def _():
-                wait(WGU.at[layer, 0, 0, pl.ds(0, (nz - 1) * rgu), :], g_par.at[slot])
+            come(q, 1, nz - 1, g_par.at[lax.rem(q, GSLOTS)])
             for h in range(1, nz):
                 piece(q, block(z + h), 2, False, lambda src, dst: to_sibling(q, src, dst))
         there, q = started(t - gdone)
@@ -421,48 +422,41 @@
         return jnp.where(zz >= nz, zz - nz, jnp.where(zz < 0, zz + nz, zz))
 
     def ring_copy(e, way, s):
-        return remote(e.buf.at[way, s, e.slot], e.buf.at[way, s + 1, e.slot], e.sent.at[way, s, e.slot], e.come.at[way, s, e.slot], (up, down)[way])
+        return remote(e.buf.at[way, s, e.slot], e.buf.at[way, s + 1, e.slot], e.sent.at[s, lax.rem(e.i, LAG + 1)], e.come.at[s, e.slot], (up, down)[way])
 
     def stage(e, s):
         def go(way):
             far = half - 1 - s + jnp.where(e.odd == way, 1, 0)
             t = terms(e, around(z + far if way == 0 else z - far))
             if s > 0:
-                wait(e.buf.at[way, s, e.slot], e.come.at[way, s - 1, e.slot])
                 t = t + e.buf[way, s, e.slot].astype(F32)
             e.buf[way, s, e.slot] = t.astype(BF16)
             ring_copy(e, way, s).start()
-        if s < half - 1:
-            @pl.when(e.valid)
-            def _():
+        @pl.when(e.valid)
+        def _():
+            if s > 0:
+                wait(e.buf.at[:, s, e.slot], e.come.at[s - 1, e.slot])
+            if s < half - 1:
                 go(0)
                 go(1)
-        else:
-            for way in (0, 1):
-                @pl.when(e.valid & (e.odd == way))
-                def _():
-                    go(way)
+            else:
+                for way in (0, 1):
+                    @pl.when(e.odd == way)
+                    def _():
+                        go(way)
 
     def stage_sent(e, s):
-        if s < half - 1:
-            @pl.when(e.valid)
-            def _():
-                ring_copy(e, 0, s).wait_send()
-                ring_copy(e, 1, s).wait_send()
-        else:
-            for way in (0, 1):
-                @pl.when(e.valid & (e.odd == way))
-                def _():
-                    ring_copy(e, way, s).wait_send()
+        @pl.when(e.valid)
+        def _():
+            wait(e.buf.at[:, s, e.slot] if s < half - 1 else e.buf.at[0, s, e.slot], e.sent.at[s, lax.rem(e.i, LAG + 1)])
 
     def last(e):
         @pl.when(e.valid)
         def _():
             t = terms(e, z)
+            wait(e.buf.at[0, half, e.slot], e.come.at[half - 1, e.slot])
             for way in (0, 1):
-                hops = half - 1 + jnp.where(e.odd == way, 1, 0)
-                wait(e.buf.at[way, hops, e.slot], e.come.at[way, hops - 1, e.slot])
-                t = t + e.buf[way, hops, e.slot].astype(F32)
+                t = t + e.buf[way, half - 1 + jnp.where(e.odd == way, 1, 0), e.slot].astype(F32)
             w = t.astype(BF16).astype(F32)
             sq = SQ[...]
             for a in range(w.shape[0] // 8):
@@ -475,8 +469,8 @@
             out[e.slot, 1] = w[rows:].astype(BF16)
             if e.gu:
                 cs = pl.ds(pl.multiple_of(e.r * cw, 128), cw)
-                pltpu.make_async_copy(FG.at[e.slot, c], ggu.at[e.layer, c, :, cs], fin_send.at[0, e.slot]).start()
-                remote(FG.at[e.slot, 1 - c], ggu.at[e.layer, c, :, cs], fin_send.at[1, e.slot], fin_recv.at[e.layer, 0], sibling).start()
+                pltpu.make_async_copy(FG.at[e.slot, c], ggu.at[e.layer, c, :, cs], fin_send.at[e.slot]).start()
+                remote(FG.at[e.slot, 1 - c], ggu.at[e.layer, c, :, cs], fin_send.at[e.slot], fin_recv.at[e.layer, 0], sibling).start()
             else:
                 for b in range(2):
                     k = 2 * e.p + b
@@ -486,19 +480,18 @@
                     owner = jnp.where(theirs, 1, 0)
                     @pl.when(owner == c)
                     def _():
-                        pltpu.make_async_copy(FD.at[e.slot, b], dst, dfin_send.at[b, e.slot]).start()
+                        pltpu.make_async_copy(FD.at[e.slot, b], dst, dfin_send.at[e.slot]).start()
                     @pl.when(owner != c)
                     def _():
-                        remote(FD.at[e.slot, b], dst, dfin_send.at[b, e.slot], fin_recv.at[e.layer, 1], sibling).start()
+                        remote(FD.at[e.slot, b], dst, dfin_send.at[e.slot], fin_recv.at[e.layer, 1], sibling).start()
 
     def last_sent(e):
         @pl.when(e.valid)
         def _():
-            for b in range(2):
-                if e.gu:
-                    wait(FG.at[e.slot, b], fin_send.at[b, e.slot])
-                else:
-                    wait(FD.at[e.slot, b], dfin_send.at[b, e.slot])
+            if e.gu:
+                wait(FG.at[e.slot], fin_send.at[e.slot])
+            else:
+                wait(FD.at[e.slot], dfin_send.at[e.slot])
 
     streams = (gu_item, d_item)
 
@@ -576,7 +569,7 @@
                 def _():
                     copy.start()
         pl.when(u != U1 - 1)(fetch)
-        @pl.when(u == 2)
+        @pl.when(u == 1)
         def _():
             normalize(H, True)
             for copy in keep:
@@ -678,9 +671,9 @@
             V((2, half + 1, SLOTS, 2 * rgu, cw), BF16), V((2, half + 1, DSLOTS, prow, d), BF16),
             V((SLOTS, 2, rgu, cw), BF16), V((DSLOTS, 2, prow // 2, d), BF16),
             V((8, 128), F32), V((n, 8, 128), F32), V((layers, CHUNKS, 2, rgu, cw), BF16), V((layers, rd, d), BF16),
-            S((4,)), S((2, 5)), S((2,)), S((2,)), S((2,)), S((GSLOTS,)), S((2, half, RSLOTS)), S((GSLOTS,)), S((GSLOTS,)), S((GSLOTS,)),
-            S, S((CHUNKS,)), S, S((2 * items,)), S((2, half, SLOTS)), S((2, half, SLOTS)), S((2, half, DSLOTS)), S((2, half, DSLOTS)),
-            S((2, SLOTS)), S((2, DSLOTS)), S((layers, 2)), S, S,
+            S((4,)), S((2, 5)), S((2,)), S((2,)), S((2,)), S((GSLOTS,)), S((half, RSLOTS)), S((GSLOTS,)), S((GSLOTS,)), S((GSLOTS,)),
+            S, S((CHUNKS,)), S, S((2 * items,)), S((half, LAG + 1)), S((half, SLOTS)), S((half, LAG + 1)), S((half, DSLOTS)),
+            S((SLOTS,)), S((DSLOTS,)), S((layers, 2)), S, S,
         ],
         compiler_params=pltpu.CompilerParams(collective_id=0, has_side_effects=True, vmem_limit_bytes=63 * 2**20),
         name="train",

time: 265 us -> 262 us (0.989)
  Pallas kernels: 255 us -> 252 us
where the time goes in v5:
time: 262 us
  Pallas kernels  252 us (96%)
  other arithmetic  8.06 us (3%)
    pallas_call x1, Pallas kernels, train(): pl.pallas_call(functools.partial(train_kernel, nz, math.isqrt(mesh.shape[...  252 us
    convert_element_type x2, other arithmetic, adamw(): return ((w - 0.02 * step).astype(BF16), m, v)  8.06 us

profile of v5, /device:TPU:21, one launch (start us, length us, event | category | flops | bytes accessed | tf_op | source)
XLA Modules:
  0.0 261.9 jit_solution(4122272076793624958)
XLA Ops:
  0.6 0.0 copy-start
  0.7 252.1 %train.1 = (bf16[2,2,40,3456]{3,2,1,0:T(8,128)(2,1)}, bf16[2,216,640]{2,1,0:T(8,128)(2,1)}, f32[1,1]{1,0:T(1,128)}, bf16[2,9,2,640,384]{4,3,2,1,0:T(8,128)(2,1)}...) custom-call(bf16[1024,640]{1,0:T(8,128)(2,1)} %bitcast.25, ...), custom_call_target="tpu_custom_call" | custom-call | tf_op jit(solution)/shard_map/train/pallas_call | solution.py:657
  253.5 0.0 copy-done
  253.5 0.0 copy-start.1
  253.5 0.0 copy-start.2
  253.5 0.0 copy-start.3
  253.5 0.0 copy-start.4
  253.5 0.0 copy-start.5
  253.5 0.0 copy-start.6
  253.5 3.8 %fusion.8 = (bf16[2,216,640]{2,1,0:T(8,128)(2,1)}, f32[2,216,640]{2,1,0:T(8,128)}, f32[2,216,640]{2,1,0:T(8,128)}) fusion(bf16[2,216,640]{2,1,0:T(8,128)(2,1)S(1)} %copy-done, f32[]{:T(128)} %bitcast.2, bf16[2,216,640]{2,1,0:T(8,128)(2,1)} %get-tuple-element.14, f32[2,216,640]{2,1,0:T(8,128)} %param.21, f32[2,216,640]{2,1,0:T(8,128)} %param.18), kind=kLoop, calls=%fused_computation.17 | loop fusion | flops 4700160 | bytes 6082564 | tf_op jit(solution)/shard_map/convert_element_type | solution.py:687
  257.3 0.0 copy-done.1
  257.3 0.0 copy-done.2
  257.3 0.0 copy-done.3
  257.3 0.0 copy-done.4
  257.3 0.0 copy-done.5
  257.3 0.2 copy-done.6
  257.5 4.3 %fusion.2 = (bf16[2,40,3456]{2,1,0:T(8,128)(2,1)}, f32[2,40,3456]{2,1,0:T(8,128)}, f32[2,40,3456]{2,1,0:T(8,128)}, bf16[2,40,3456]{2,1,0:T(8,128)(2,1)}, f32[2,40,3456]{2,1,0:T(8,128)}, /*index=5*/f32[2,40,3456]{2,1,0:T(8,128)}) fusion(bf16[2,40,3456]{2,1,0:T(8,128)(2,1)S(1)} %copy-done.1, f32[]{:T(128)} %bitcast.2, f32[2,40,3456]{2,1,0:T(8,128)S(1)} %copy-done.3, ...), kind=kLoop, calls=%fused_computation.11 | loop fusion | flops 9400320 | bytes 12165124 | tf_op jit(solution)/shard_map/convert_element_type | solution.py:687
Async XLA Ops:
  0.6 252.8 %copy-start = (bf16[2,216,640]{2,1,0:T(8,128)(2,1)S(1)}, bf16[2,216,640]{2,1,0:T(8,128)(2,1)}, u32[]{:S(2)}) copy-start(bf16[2,216,640]{2,1,0:T(8,128)(2,1)} %wd.1) | copy-start | bytes 1658884
  253.5 3.8 %copy-start.1 = (bf16[2,40,3456]{2,1,0:T(8,128)(2,1)S(1)}, bf16[2,40,3456]{2,1,0:T(8,128)(2,1)}, u32[]{:S(2)}) copy-start(bf16[2,40,3456]{2,1,0:T(8,128)(2,1)} %wg.1) | copy-start | bytes 1658884
  253.5 3.8 %copy-start.2 = (bf16[2,40,3456]{2,1,0:T(8,128)(2,1)S(1)}, bf16[2,40,3456]{2,1,0:T(8,128)(2,1)}, u32[]{:S(2)}) copy-start(bf16[2,40,3456]{2,1,0:T(8,128)(2,1)} %wu.1) | copy-start | bytes 1658884
  253.5 3.8 %copy-start.3 = (f32[2,40,3456]{2,1,0:T(8,128)S(1)}, f32[2,40,3456]{2,1,0:T(8,128)}, u32[]{:S(2)}) copy-start(f32[2,40,3456]{2,1,0:T(8,128)} %param.19) | copy-start | bytes 3317764
  253.5 3.8 %copy-start.4 = (f32[2,40,3456]{2,1,0:T(8,128)S(1)}, f32[2,40,3456]{2,1,0:T(8,128)}, u32[]{:S(2)}) copy-start(f32[2,40,3456]{2,1,0:T(8,128)} %param.16) | copy-start | bytes 3317764
  253.5 3.8 %copy-start.5 = (f32[2,40,3456]{2,1,0:T(8,128)S(1)}, f32[2,40,3456]{2,1,0:T(8,128)}, u32[]{:S(2)}) copy-start(f32[2,40,3456]{2,1,0:T(8,128)} %param.20) | copy-start | bytes 3317764
  253.5 4.0 %copy-start.6 = (f32[2,40,3456]{2,1,0:T(8,128)S(1)}, f32[2,40,3456]{2,1,0:T(8,128)}, u32[]{:S(2)}) copy-start(f32[2,40,3456]{2,1,0:T(8,128)} %param.17) | copy-start | bytes 3317764

commit v6 on v5

--- a/solution.py
+++ b/solution.py
@@ -687,17 +687,40 @@
     return (w - 0.02 * step).astype(BF16), m, v
 
 
+def update_kernel(count, squares, ggu, gd, *refs):
+    ins, outs = refs[:9], refs[9:]
+    mean = jnp.full((8, 128), squares[0, 0] * (1.0 / count), F32)
+    factor = jnp.minimum(1.0, 0.5 * lax.rsqrt(mean + 1e-30))[:1, :1]
+    for i, g in enumerate((ggu[0, 0], ggu[0, 1], gd[0])):
+        w, m, v = (ins[i + 3 * k][0].astype(F32) for k in range(3))
+        for k, one in enumerate(adamw(w, m, v, g.astype(F32) * factor)):
+            outs[i + 3 * k][0] = one
+
+
+def update(n, squares, ggu, gd, arrays):
+    layers, _, rgu, ff = ggu.shape
+    rd, d = gd.shape[1:]
+    wide = pl.BlockSpec((1, rgu, ff), lambda i: (i, 0, 0))
+    tall = pl.BlockSpec((1, rd, d), lambda i: (i, 0, 0))
+    both = pl.BlockSpec((1, 2, rgu, ff), lambda i: (i, 0, 0, 0))
+    specs = [wide, wide, tall] * 3
+    size = ggu.size + gd.size
+    return pl.pallas_call(
+        functools.partial(update_kernel, n * size),
+        grid=(layers,),
+        out_shape=[jax.ShapeDtypeStruct(a.shape, a.dtype) for a in arrays],
+        in_specs=[pl.BlockSpec(memory_space=pltpu.SMEM), both, tall] + specs,
+        out_specs=specs,
+        compiler_params=pltpu.CompilerParams(vmem_limit_bytes=60 * 2**20),
+        cost_estimate=pl.CostEstimate(flops=20 * size, transcendentals=size, bytes_accessed=22 * size),
+        name="update",
+    )(squares, ggu, gd, *arrays)
+
+
 def solution(mesh):
-    n = mesh.shape["dp"]
-
     def step(x, dy, *arrays):
-        weights, m, v = (arrays[i : i + 3] for i in (0, 3, 6))
-        ggu, gd, squares = train(mesh, x[0], dy[0], *weights)[:3]
-        gradients = [g.astype(F32) for g in (ggu[:, 0], ggu[:, 1], gd)]
-        count = n * sum(g.size for g in gradients)
-        factor = jnp.minimum(1.0, 0.5 * lax.rsqrt(squares[0, 0] / count + 1e-30))
-        new = [adamw(w.astype(F32), m, v, g * factor) for w, m, v, g in zip(weights, m, v, gradients, strict=True)]
-        return tuple(one[which] for which in range(3) for one in new)
+        ggu, gd, squares = train(mesh, x[0], dy[0], *arrays[:3])[:3]
+        return tuple(update(mesh.shape["dp"], squares, ggu, gd, arrays))
 
     states, cut = P(("rep", "dp"), None, None), P(None, "dp", None)
     return jax.shard_map(

time: 262 us -> 260 us (level)
  other arithmetic: 8.06 us -> 0 us
  Pallas kernels: 252 us -> 259 us
    convert_element_type x2 -> x0, other arithmetic: 8.06 us -> none  [adamw(): return ((w - 0.02 * step).astype(BF16), m, v)]
    pallas_call x0 -> x1, Pallas kernels: none -> 7.38 us  [update(): pl.pallas_call(functools.partial(update_kernel, n * size), grid=(layers,)...]
where the time goes in v6:
time: 260 us
  Pallas kernels  259 us (100%)
    pallas_call x1, Pallas kernels, train(): pl.pallas_call(functools.partial(train_kernel, nz, math.isqrt(mesh.shape[...  252 us
    pallas_call x1, Pallas kernels, update(): pl.pallas_call(functools.partial(update_kernel, n * size), grid=(layers,)...  7.38 us

profile of v6, /device:TPU:21, one launch (start us, length us, event | category | flops | bytes accessed | tf_op | source)
XLA Modules:
  0.0 260.1 jit_solution(3321037961015358839)
XLA Ops:
  0.6 252.0 %train.1 = (bf16[2,2,40,3456]{3,2,1,0:T(8,128)(2,1)}, bf16[2,216,640]{2,1,0:T(8,128)(2,1)}, f32[1,1]{1,0:T(1,128)}, bf16[2,9,2,640,384]{4,3,2,1,0:T(8,128)(2,1)}...) custom-call(bf16[1024,640]{1,0:T(8,128)(2,1)} %bitcast.2, ...), custom_call_target="tpu_custom_call" | custom-call | tf_op jit(solution)/shard_map/train/pallas_call | solution.py:657
  252.7 7.4 %update.1 = (bf16[2,40,3456]{2,1,0:T(8,128)(2,1)}, bf16[2,40,3456]{2,1,0:T(8,128)(2,1)}, bf16[2,216,640]{2,1,0:T(8,128)(2,1)}, f32[2,40,3456]{2,1,0:T(8,128)}, f...) custom-call(f32[1,1]{1,0:T(1,128)} %get-tuple-element.12.squares, ...), custom_call_target="tpu_custom_call" | custom-call | flops 16588800 | bytes 18247680 | tf_op jit(solution)/shard_map/update/pallas_call | solution.py:708
